TPU v7x, 256 devices: a whole 4x4x8 slice. The times are simulated.
256 devices in a mesh: section: 2 (over core), dp: 16 (over z, x_lo), tensor: 8 (over y, x_hi).
Axes of the slice: x: 4 (x_hi: 2, x_lo: 2; x = x_hi * 2 + x_lo), y: 4, z: 8, core: 2. Of those that a mesh axis runs over, the one named last changes fastest.
Arguments:
- tokens: bfloat16 [2048, 4096], P('dp', 'tensor'), may hold values from -6 to 6
- gain: bfloat16 [2, 4096], P('section', 'tensor'), may hold values from 0.099609375 to 1.8984375
- w_up: bfloat16 [2, 4096, 5120], P('section', 'dp', 'tensor'), may hold values from -0.09375 to 0.09375
- w_down: bfloat16 [2, 5120, 4096], P('section', 'tensor', 'dp'), may hold values from -0.078125 to 0.078125
- cotangent: bfloat16 [2, 2048, 4096], P('section', 'dp'), may hold values from -6 to 6
Outputs:
- states: bfloat16 [2, 2048, 4096], P('section', 'dp', 'tensor')
- grad_down: bfloat16 [2, 5120, 4096], P('section', 'tensor', 'dp')
All inputs are finite; a program needn't handle non-finite values.
Results may differ from a plain program's by a relative error of at most 0.02.
Values may be sent and summed in bfloat16 or wider, within the bound.
A program may use at most 64 MiB of HBM per device.

v0:
```python
import jax
import jax.numpy as jnp
from jax import lax
from jax.sharding import Mesh
from jax.sharding import PartitionSpec as P

MICRO = 2
MB_ROWS = 64
DP = ("dp_0", "dp_1")


EPS = 1e-06


def gathered_by_axis(array, axes, dim):
    filled = array
    for number in range(len(axes) - 1, -1, -1):
        filled = lax.all_gather(filled, axes[number], axis=dim, tiled=True)
    return filled


def in_order(pieces, dim):
    dims = list(pieces.shape[1:])
    dims[dim] *= pieces.shape[0]
    return jnp.moveaxis(pieces, 0, dim).reshape(dims)


def copy_for_each(array, axis):
    peers = lax.axis_size(axis)
    return lax.all_to_all(
        jnp.broadcast_to(array[None], (peers, *array.shape)), axis, 0, 0, tiled=True
    )


def collect(array, axis, dim):
    return in_order(copy_for_each(array, axis), dim)


def split_up(array, dim, peers):
    before, after = (array.shape[:dim], array.shape[dim + 1 :])
    return jnp.moveaxis(array.reshape(*before, peers, -1, *after), dim, 0)


def summed_on_arrival(array, axis, dim):
    pieces = split_up(array, dim, lax.axis_size(axis))
    arrived = lax.all_to_all(pieces, axis, split_axis=0, concat_axis=0, tiled=True)
    return arrived.astype(jnp.float32).sum(axis=0)


def shifted(array, axis, by):
    peers = lax.axis_size(axis)
    pairs = [(i, i + by) for i in range(peers) if 0 <= i + by < peers]
    return lax.ppermute(array, axis, pairs)


def body(tokens, gain, w_up, w_down, cotangent):
    section_id = lax.axis_index("section")
    section_count = lax.axis_size("section")
    up_whole = gathered_by_axis(w_up[0], DP, 0)
    down_whole = gathered_by_axis(w_down[0], DP, 1)
    width = up_whole.shape[0]
    hidden_width = up_whole.shape[1]
    gain_own = gain[0]
    gain_whole = lax.all_gather(gain_own, "tensor", axis=0, tiled=True)
    micro_rows = MB_ROWS
    micro_count = MICRO
    own_width = tokens.shape[1]
    tok_rows = tokens.shape[0]

    def project(normed):
        pre_act = jnp.dot(normed, up_whole, preferred_element_type=jnp.float32)
        hidden = jax.nn.gelu(pre_act, approximate=True).astype(jnp.bfloat16)
        partial_value = jnp.dot(hidden, down_whole, preferred_element_type=jnp.float32).astype(
            jnp.bfloat16
        )
        return (hidden, lax.optimization_barrier(partial_value).astype(jnp.float32))

    def skipped(normed):
        return (
            jnp.zeros((micro_rows, hidden_width), jnp.bfloat16),
            jnp.zeros((micro_rows, width), jnp.float32),
        )

    def advance(step_id, loop_state):
        incoming, states, hiddens = loop_state
        micro_id = step_id - section_id
        active = (micro_id >= 0) & (micro_id < micro_count)
        slot_pos = jnp.clip(micro_id, 0, micro_count - 1) * micro_rows
        entry_rows = lax.dynamic_slice_in_dim(tokens, slot_pos, micro_rows, 0)
        current = jnp.where(section_id == 0, entry_rows, incoming)
        current_f = current.astype(jnp.float32)
        whole_rows = collect(current, "tensor", 1)
        whole_f = whole_rows.astype(jnp.float32)
        inverse_rms = lax.rsqrt(jnp.mean(whole_f * whole_f, axis=1, keepdims=True) + EPS)
        normed = (whole_f * inverse_rms * gain_whole.astype(jnp.float32)).astype(jnp.bfloat16)
        hidden, partial_value = lax.cond(active, project, skipped, normed)
        summed = summed_on_arrival(partial_value.astype(jnp.bfloat16), "tensor", 1)
        result = (current_f + summed).astype(jnp.bfloat16)
        old_state = lax.dynamic_slice_in_dim(states, slot_pos, micro_rows, 0)
        states = lax.dynamic_update_slice_in_dim(
            states, jnp.where(active, result, old_state), slot_pos, 0
        )
        old_hidden = lax.dynamic_slice_in_dim(hiddens, slot_pos, micro_rows, 0)
        hiddens = lax.dynamic_update_slice_in_dim(
            hiddens, jnp.where(active, hidden, old_hidden), slot_pos, 0
        )
        incoming = shifted(result, "section", 1)
        return (incoming, states, hiddens)

    initial = (
        jnp.zeros((micro_rows, own_width), jnp.bfloat16),
        jnp.zeros((tok_rows, own_width), jnp.bfloat16),
        jnp.zeros((tok_rows, hidden_width), jnp.bfloat16),
    )
    final_state = lax.fori_loop(0, micro_count + section_count - 1, advance, initial)
    states = final_state[1]
    hiddens = final_state[2]
    cot_own = cotangent[0]
    dp_count = lax.axis_size(DP)
    hidden_all = lax.all_gather(hiddens, DP, axis=0, tiled=True)
    cot_mine = lax.all_to_all(cot_own, DP, split_axis=1, concat_axis=0, tiled=True)
    grad_own = jnp.zeros((hidden_width, width // dp_count), jnp.float32)
    for peer_id in range(dp_count):
        lower = peer_id * tok_rows
        partial_value = lax.dot_general(
            hidden_all[lower : lower + tok_rows],
            cot_mine[lower : lower + tok_rows],
            (((0,), (0,)), ((), ())),
            preferred_element_type=jnp.float32,
        ).astype(jnp.bfloat16)
        grad_own = grad_own + lax.optimization_barrier(partial_value).astype(jnp.float32)
    return (states[None], grad_own.astype(jnp.bfloat16)[None])


def solution(mesh):
    torus = Mesh(
        mesh.devices.reshape(mesh.shape["section"], 8, 2, mesh.shape["tensor"]),
        ("section", "dp_0", "dp_1", "tensor"),
    )
    in_specs = (
        P(DP, "tensor"),
        P("section", "tensor"),
        P("section", DP, "tensor"),
        P("section", "tensor", DP),
        P("section", DP, None),
    )
    out_specs = (P("section", DP, "tensor"), P("section", "tensor", DP))
    return jax.shard_map(body, mesh=torus, in_specs=in_specs, out_specs=out_specs, check_vma=False)
```

profile of v0, /device:TPU:1, one launch (start us, length us, event | category | flops | bytes accessed | tf_op | source)
XLA Modules:
  0.0 372.1 jit_solution(14900252217565980653)
XLA Ops:
  7.2 11.5 %all-gather.1 = bf16[1,512,640]{2,1,0:T(8,128)(2,1)} all-gather(bf16[1,256,640]{2,1,0:T(8,128)(2,1)} %param.11), channel_id=3, replica_groups=mesh['section'=2,'dp_0'=8,'dp_1'=2,'tensor'=8] {'dp_1'}, dimensions={1}, use_global_device_ids=true | all-gather | bytes 983040 | tf_op jit(solution)/shard_map/all_gather | solution.py:18
  18.8 8.4 %all-gather.3 = bf16[1,640,512]{2,1,0:T(8,128)(2,1)} all-gather(bf16[1,640,256]{2,1,0:T(8,128)(2,1)} %param.12), channel_id=5, replica_groups=mesh['section'=2,'dp_0'=8,'dp_1'=2,'tensor'=8] {'dp_1'}, dimensions={2}, use_global_device_ids=true | all-gather | bytes 983040 | tf_op jit(solution)/shard_map/all_gather | solution.py:18
  27.3 28.3 %all-gather = bf16[1,4096]{1,0:T(2,128)(2,1)S(1)} all-gather(bf16[1,512]{1,0:T(2,128)(2,1)S(1)} %copy-done.7), channel_id=2, replica_groups=mesh['section'=2,'dp_0'=8,'dp_1'=2,'tensor'=8] {'tensor'}, dimensions={1}, use_global_device_ids=true | all-gather | bytes 9216 | tf_op jit(solution)/shard_map/all_gather | solution.py:64
  55.6 31.5 %all-gather.11.cloned.1.call-done = bf16[1,4096,640]{2,1,0:T(8,128)(2,1)} async-done(((bf16[1,512,640]{2,1,0:T(8,128)(2,1)}), bf16[1,4096,640]{2,1,0:T(8,128)(2,1)}) %all-gather.11.cloned.1.call-update) | async-done | bytes 5242896 | tf_op jit(solution)/shard_map/all_gather | solution.py:18
  87.2 65.0 %all-gather.13.cloned.1.call-done = bf16[1,640,4096]{2,1,0:T(8,128)(2,1)} async-done(((bf16[1,640,512]{2,1,0:T(8,128)(2,1)}), bf16[1,640,4096]{2,1,0:T(8,128)(2,1)}) %all-gather.13.cloned.1.call-update) | async-done | bytes 5242896 | tf_op jit(solution)/shard_map/all_gather | solution.py:18
  152.2 126.2 %while.18 = (s32[]{:T(128)}, bf16[64,512]{1,0:T(8,128)(2,1)S(1)}, bf16[128,512]{1,0:T(8,128)(2,1)S(1)}, bf16[128,640]{1,0:T(8,128)(2,1)S(1)}, pred[]{:T(512)}, /...) while((s32[]{:T(128)}, bf16[64,512]{1,0:T(8,128)(2,1)S(1)}, ...), condition=%wide.region_5.6_spmd, body=%wide.region_0.5_spmd.sunk | while | flops 674254912 | bytes 67036620 | solution.py:115
  153.1 6.4 %all-to-all-start = ((bf16[8,64,512]{2,1,0:T(8,128)(2,1)}), bf16[8,64,512]{2,1,0:T(8,128)(2,1)S(1)}, u32[]{:S(2)}, u32[]{:S(2)}) async-start(bf16[8,64,512]{2,1,0:T(8,128)(2,1)} %broadcast_in_dim.44), calls=%async_computation | async-start | bytes 1048576 | tf_op jit(solution)/shard_map/while/body/eval_jaxpr/all_to_all | solution.py:30
  159.6 10.6 %all-to-all-done = bf16[8,64,512]{2,1,0:T(8,128)(2,1)S(1)} async-done(((bf16[8,64,512]{2,1,0:T(8,128)(2,1)}), bf16[8,64,512]{2,1,0:T(8,128)(2,1)S(1)}, u32[]{:S(2)}, u32[]{:S(2)}) %all-to-all-start) | async-done | bytes 524320 | tf_op jit(solution)/shard_map/while/body/eval_jaxpr/all_to_all | solution.py:30
  170.7 2.1 copy-done
  173.7 1.0 copy.67
  174.7 3.5 all-to-all-start.1
  178.2 9.0 %all-to-all-done.1 = bf16[8,64,512]{2,1,0:T(8,128)(2,1)S(1)} async-done(((bf16[8,64,512]{2,1,0:T(8,128)(2,1)}), bf16[8,64,512]{2,1,0:T(8,128)(2,1)S(1)}, u32[]{:S(2)}, u32[]{:S(2)}) %all-to-all-start.1) | async-done | bytes 524320 | tf_op jit(solution)/shard_map/while/body/eval_jaxpr/all_to_all | solution.py:46
  187.3 1.3 collective-permute-start
  188.6 7.6 %collective-permute-done = bf16[64,512]{1,0:T(8,128)(2,1)S(1)} collective-permute-done((bf16[64,512]{1,0:T(8,128)(2,1)S(1)}, bf16[64,512]{1,0:T(8,128)(2,1)S(1)}, u32[]{:S(2)}, u32[]{:S(2)}) %collective-permute-start) | collective-permute-done | bytes 65568 | tf_op jit(solution)/shard_map/while/body/eval_jaxpr/ppermute | solution.py:53
  197.1 3.5 all-to-all-start
  200.6 11.0 %all-to-all-done = bf16[8,64,512]{2,1,0:T(8,128)(2,1)S(1)} async-done(((bf16[8,64,512]{2,1,0:T(8,128)(2,1)}), bf16[8,64,512]{2,1,0:T(8,128)(2,1)S(1)}, u32[]{:S(2)}, u32[]{:S(2)}) %all-to-all-start) | async-done | bytes 524320 | tf_op jit(solution)/shard_map/while/body/eval_jaxpr/all_to_all | solution.py:30
  212.2 2.1 copy-done
  214.3 4.5 %conditional.2 = (bf16[64,640]{1,0:T(8,128)(2,1)}, bf16[64,4096]{1,0:T(8,128)(2,1)S(1)}) conditional(s32[]{:T(128)} %convert_element_type.313, () %tuple.49, (bf16[64,4096]{1,0:T(8,128)(2,1)S(1)}, bf16[4096,640]{1,0:T(8,128)(2,1)S(1)}, bf16[640,4096]{1,0:T(8,128)(2,1)}) %tuple.63), branch_computations={%region_2.2_spmd, %region_3.3_spmd} | conditional | flops 671719424 | bytes 32669740 | solution.py:96
  214.3 1.7 fusion.7
  216.0 0.9 copy-done.1
  216.9 1.9 convolution_convert_fusion
  219.0 1.0 copy.67
  219.9 3.5 all-to-all-start.1
  223.4 10.2 %all-to-all-done.1 = bf16[8,64,512]{2,1,0:T(8,128)(2,1)S(1)} async-done(((bf16[8,64,512]{2,1,0:T(8,128)(2,1)}), bf16[8,64,512]{2,1,0:T(8,128)(2,1)S(1)}, u32[]{:S(2)}, u32[]{:S(2)}) %all-to-all-start.1) | async-done | bytes 524320 | tf_op jit(solution)/shard_map/while/body/eval_jaxpr/all_to_all | solution.py:46
  233.8 1.3 collective-permute-start
  235.1 0.9 select_dynamic-update-slice_fusion.5
  236.0 2.1 collective-permute-done
  238.9 3.5 all-to-all-start
  242.4 11.0 %all-to-all-done = bf16[8,64,512]{2,1,0:T(8,128)(2,1)S(1)} async-done(((bf16[8,64,512]{2,1,0:T(8,128)(2,1)}), bf16[8,64,512]{2,1,0:T(8,128)(2,1)S(1)}, u32[]{:S(2)}, u32[]{:S(2)}) %all-to-all-start) | async-done | bytes 524320 | tf_op jit(solution)/shard_map/while/body/eval_jaxpr/all_to_all | solution.py:30
  254.1 2.1 copy-done
  256.2 4.5 %conditional.2 = (bf16[64,640]{1,0:T(8,128)(2,1)}, bf16[64,4096]{1,0:T(8,128)(2,1)S(1)}) conditional(s32[]{:T(128)} %convert_element_type.313, () %tuple.49, (bf16[64,4096]{1,0:T(8,128)(2,1)S(1)}, bf16[4096,640]{1,0:T(8,128)(2,1)S(1)}, bf16[640,4096]{1,0:T(8,128)(2,1)}) %tuple.63), branch_computations={%region_2.2_spmd, %region_3.3_spmd} | conditional | flops 671719424 | bytes 32669740 | solution.py:96
  256.2 1.7 fusion.7
  257.9 0.9 copy-done.1
  258.7 1.9 convolution_convert_fusion
  260.9 1.0 copy.67
  261.8 3.5 all-to-all-start.1
  265.3 9.9 %all-to-all-done.1 = bf16[8,64,512]{2,1,0:T(8,128)(2,1)S(1)} async-done(((bf16[8,64,512]{2,1,0:T(8,128)(2,1)}), bf16[8,64,512]{2,1,0:T(8,128)(2,1)S(1)}, u32[]{:S(2)}, u32[]{:S(2)}) %all-to-all-start.1) | async-done | bytes 524320 | tf_op jit(solution)/shard_map/while/body/eval_jaxpr/all_to_all | solution.py:46
  275.3 1.3 collective-permute-start
  276.6 0.9 select_dynamic-update-slice_fusion.5
  277.5 0.9 collective-permute-done
  279.8 42.9 %all_to_all.38 = bf16[128,16,256]{0,2,1:T(8,128)(2,1)S(1)} all-to-all(bf16[128,16,256]{0,2,1:T(8,128)(2,1)S(1)} %bitcast.112), channel_id=1, replica_groups=mesh['section'=2,'dp_0'=8,'dp_1'=2,'tensor'=8] {'dp_0','dp_1'}, dimensions={1} | all-to-all | bytes 2097152 | tf_op jit(solution)/shard_map/all_to_all | solution.py:121
  322.8 32.1 %all-gather.9.cloned.1.call-done = bf16[2048,640]{1,0:T(8,128)(2,1)} async-done(((bf16[128,640]{1,0:T(8,128)(2,1)}), bf16[2048,640]{1,0:T(8,128)(2,1)}) %all-gather.9.cloned.1.call-update) | async-done | bytes 2621456 | tf_op jit(solution)/shard_map/all_gather | solution.py:120
  354.8 1.3 convolution_convert_fusion.1
  356.2 1.2 convolution_convert_fusion.2
  357.4 1.2 convolution_convert_fusion.3
  358.6 1.2 convolution_convert_fusion.4
  359.8 1.2 convolution_convert_fusion.5
  364.1 1.5 fusion.9
  (76 shorter events, 11.3 us)
Async XLA Ops:
  7.2 20.1 %copy-start.7 = (bf16[1,512]{1,0:T(2,128)(2,1)S(1)}, bf16[1,512]{1,0:T(2,128)(2,1)}, u32[]{:S(2)}) copy-start(bf16[1,512]{1,0:T(2,128)(2,1)} %param.10) | copy-start | bytes 3076
  7.2 145.0 %copy-start.6 = (bf16[128,512]{1,0:T(8,128)(2,1)S(1)}, bf16[128,512]{1,0:T(8,128)(2,1)}, u32[]{:S(2)}) copy-start(bf16[128,512]{1,0:T(8,128)(2,1)} %param.9) | copy-start | bytes 393220
  7.2 80.0 %all-gather.11.cloned.1.call-start = ((), (), s32[]{:S(2)}) async-start(), calls=%async_computation.4 | async-start | bytes 5898240 | tf_op jit(solution)/shard_map/all_gather | solution.py:18
  18.7 133.4 %all-gather.13.cloned.1.call-start = ((), (), s32[]{:S(2)}) async-start(), calls=%async_computation.5 | async-start | bytes 5898240 | tf_op jit(solution)/shard_map/all_gather | solution.py:18
  27.2 327.6 %all-gather.9.cloned.1.call-start = ((), (), s32[]{:S(2)}) async-start(), calls=%async_computation.3 | async-start | bytes 2785280 | tf_op jit(solution)/shard_map/all_gather | solution.py:120
  152.2 126.9 %copy-start.5 = (bf16[1,128,4096]{2,1,0:T(8,128)(2,1)S(1)}, bf16[1,128,4096]{2,1,0:T(8,128)(2,1)}, u32[]{:S(2)}) copy-start(bf16[1,128,4096]{2,1,0:T(8,128)(2,1)} %param.13) | copy-start | bytes 3145732
  153.1 17.0 %all-to-all-start = ((bf16[8,64,512]{2,1,0:T(8,128)(2,1)}), bf16[8,64,512]{2,1,0:T(8,128)(2,1)S(1)}, u32[]{:S(2)}, u32[]{:S(2)}) async-start(bf16[8,64,512]{2,1,0:T(8,128)(2,1)} %broadcast_in_dim.44), calls=%async_computation | async-start | bytes 1048576 | tf_op jit(solution)/shard_map/while/body/eval_jaxpr/all_to_all | solution.py:30
  170.3 2.5 copy-start
  174.7 12.5 %all-to-all-start.1 = ((bf16[8,64,512]{2,1,0:T(8,128)(2,1)}), bf16[8,64,512]{2,1,0:T(8,128)(2,1)S(1)}, u32[]{:S(2)}, u32[]{:S(2)}) async-start(bf16[8,64,512]{2,1,0:T(8,128)(2,1)} %copy.67), calls=%async_computation.1 | async-start | bytes 1048576 | tf_op jit(solution)/shard_map/while/body/eval_jaxpr/all_to_all | solution.py:46
  187.3 8.9 %collective-permute-start = (bf16[64,512]{1,0:T(8,128)(2,1)S(1)}, bf16[64,512]{1,0:T(8,128)(2,1)S(1)}, u32[]{:S(2)}, u32[]{:S(2)}) collective-permute-start(bf16[64,512]{1,0:T(8,128)(2,1)S(1)} %get-tuple-element.299), channel_id=1, source_target_pairs={{0,128},{1,129},{2,130},{3,131},{4,132},{5,133},{6,134},{7,135},{8... | collective-permute-start | bytes 196616 | tf_op jit(solution)/shard_map/while/body/eval_jaxpr/ppermute | solution.py:53
  197.1 14.6 %all-to-all-start = ((bf16[8,64,512]{2,1,0:T(8,128)(2,1)}), bf16[8,64,512]{2,1,0:T(8,128)(2,1)S(1)}, u32[]{:S(2)}, u32[]{:S(2)}) async-start(bf16[8,64,512]{2,1,0:T(8,128)(2,1)} %broadcast_in_dim.44), calls=%async_computation | async-start | bytes 1048576 | tf_op jit(solution)/shard_map/while/body/eval_jaxpr/all_to_all | solution.py:30
  211.8 2.5 copy-start
  214.3 2.5 copy-start.1
  219.9 13.7 %all-to-all-start.1 = ((bf16[8,64,512]{2,1,0:T(8,128)(2,1)}), bf16[8,64,512]{2,1,0:T(8,128)(2,1)S(1)}, u32[]{:S(2)}, u32[]{:S(2)}) async-start(bf16[8,64,512]{2,1,0:T(8,128)(2,1)} %copy.67), calls=%async_computation.1 | async-start | bytes 1048576 | tf_op jit(solution)/shard_map/while/body/eval_jaxpr/all_to_all | solution.py:46
  233.8 4.3 %collective-permute-start = (bf16[64,512]{1,0:T(8,128)(2,1)S(1)}, bf16[64,512]{1,0:T(8,128)(2,1)S(1)}, u32[]{:S(2)}, u32[]{:S(2)}) collective-permute-start(bf16[64,512]{1,0:T(8,128)(2,1)S(1)} %get-tuple-element.299), channel_id=1, source_target_pairs={{0,128},{1,129},{2,130},{3,131},{4,132},{5,133},{6,134},{7,135},{8... | collective-permute-start | bytes 196616 | tf_op jit(solution)/shard_map/while/body/eval_jaxpr/ppermute | solution.py:53
  238.9 14.6 %all-to-all-start = ((bf16[8,64,512]{2,1,0:T(8,128)(2,1)}), bf16[8,64,512]{2,1,0:T(8,128)(2,1)S(1)}, u32[]{:S(2)}, u32[]{:S(2)}) async-start(bf16[8,64,512]{2,1,0:T(8,128)(2,1)} %broadcast_in_dim.44), calls=%async_computation | async-start | bytes 1048576 | tf_op jit(solution)/shard_map/while/body/eval_jaxpr/all_to_all | solution.py:30
  253.7 2.5 copy-start
  256.2 2.5 copy-start.1
  261.8 13.4 %all-to-all-start.1 = ((bf16[8,64,512]{2,1,0:T(8,128)(2,1)}), bf16[8,64,512]{2,1,0:T(8,128)(2,1)S(1)}, u32[]{:S(2)}, u32[]{:S(2)}) async-start(bf16[8,64,512]{2,1,0:T(8,128)(2,1)} %copy.67), calls=%async_computation.1 | async-start | bytes 1048576 | tf_op jit(solution)/shard_map/while/body/eval_jaxpr/all_to_all | solution.py:46
  275.3 3.1 collective-permute-start
  278.4 0.7 copy-start.2
  278.5 78.9 %copy-start.4 = (bf16[128,512]{1,0:T(8,128)(2,1)}, bf16[128,512]{1,0:T(8,128)(2,1)S(1)}, u32[]{:S(2)}) copy-start(bf16[128,512]{1,0:T(8,128)(2,1)S(1)} %get-tuple-element.209) | copy-start | bytes 393220
  354.8 6.1 %copy-start.3 = (bf16[2048,640]{1,0:T(8,128)(2,1)S(1)}, bf16[2048,640]{1,0:T(8,128)(2,1)}, u32[]{:S(2)}) copy-start(bf16[2048,640]{1,0:T(8,128)(2,1)} %all-gather.9.cloned.1.call-done) | copy-start | bytes 7864324
Sparse Core Ops, SparseCore 0:
  18.9 68.2 all-gather.10
  88.9 63.1 all-gather.12
  279.3 75.5 all-gather.8
where the time goes:
time: 378 us; the launch traced here: 372 us
  waiting for transfers between devices  201 us (53%)
  blocking collectives  91.1 us (24%)
  starting transfers between devices  27.9 us (7%)
  matrix products  16.4 us (4%)
  local copies, waits for them, and re-layouts  16.2 us (4%)
  between operations  14 us (4%)
  other arithmetic  5.32 us (1%)
    all_gather x2, waiting for transfers between devices, gathered_by_axis(): filled = lax.all_gather(filled, axes[number], axis=dim, tiled=True)  96.5 us
    all_to_all x1, blocking collectives, body(): lax.all_to_all(cot_own, DP, split_axis=1, concat_axis=0, tiled=True)  42.9 us
    all_to_all x3, waiting for transfers between devices, copy_for_each(): lax.all_to_all(jnp.broadcast_to(array[None], (peers, *array.shape)), axis...  32.7 us
    all_gather x1, waiting for transfers between devices, body(): hidden_all = lax.all_gather(hiddens, DP, axis=0, tiled=True)  32.1 us
    all_to_all x3, waiting for transfers between devices, summed_on_arrival(): lax.all_to_all(pieces, axis, split_axis=0, concat_axis=0, tiled=True)  29.1 us
    all_gather x1, blocking collectives, body(): gain_whole = lax.all_gather(gain_own, 'tensor', axis=0, tiled=True)  28.3 us
    all_gather x2, blocking collectives, gathered_by_axis(): filled = lax.all_gather(filled, axes[number], axis=dim, tiled=True)  19.9 us
    all_to_all x3, starting transfers between devices, copy_for_each(): lax.all_to_all(jnp.broadcast_to(array[None], (peers, *array.shape)), axis...  13.4 us
  transfers between devices with their start and end apart: 12, of which 12 were waited for; matrix products, arithmetic and copies ran while one was open for 1% of the time, Pallas kernels for 0%

commit v1 on v0

v1 whole, which is shorter than its diff:
```python
import jax
import jax.numpy as jnp
from jax import lax
from jax.experimental import pallas as pl
from jax.experimental.pallas import tpu as pltpu
from jax.sharding import Mesh
from jax.sharding import PartitionSpec as P

EPS = 1e-06
MESH = pl.DeviceIdType.MESH
NZ, NY, NX = 8, 4, 2
NT = NY * NX
F32, BF16 = jnp.float32, jnp.bfloat16


def ring_offset(i):
    return ((i + 1) // 2) * (1 - 2 * ((i + 1) % 2))


def kernel(
    width,
    tok_ref, gain_ref, up_ref, down_ref, cot_ref,
    state_ref, grad_ref,
    x_all, c_all, gain_z, up_pair, down_pair,
    part_out, part_in, sq_out, sq_in, acc, hid_all, y_out, y_in, x_next,
    grad_own, grad_out, grad_in,
    xin_s, xin_r, gain_s, gain_r, cotp_s, cotp_r, up_s, up_r, down_s, down_r, core_s,
    ag_s, ag_r, cg_s, cg_r, rz_s, rz_r, sq_s, sq_r, az_s, az_r, rt_s, rt_r,
    gr_s, gr_r, out_s, out_r,
):
    section = lax.axis_index("section")
    z = lax.axis_index("z")
    xl = lax.axis_index("xl")
    y = lax.axis_index("y")
    xh = lax.axis_index("xh")
    t = y * NX + xh
    half = up_ref.shape[1]
    feats = tok_ref.shape[1]
    pair = {"xl": 1 - xl}
    core = {"section": 1 - section}
    mirror = {"z": t, "y": z // NX, "xh": z % NX}
    off_diag = z != t

    def to_tensor(k):
        return {"y": k // NX, "xh": k % NX}

    def tensor_at(i):
        k = i % NY
        step = k + (k // 2) * (1 - 2 * (k % 2))
        return ((y + step) % NY) * NX + (xh + i // NY) % NX

    def z_at(i):
        return (z + ring_offset(i) + NZ) % NZ

    def rdma(src, dst, ssem, rsem, dev):
        return pltpu.make_async_remote_copy(
            src_ref=src, dst_ref=dst, send_sem=ssem, recv_sem=rsem,
            device_id=dev, device_id_type=MESH,
        )

    barrier = pltpu.get_barrier_semaphore()

    @pl.loop(1, NZ)
    def _(i):
        pl.semaphore_signal(barrier, inc=1, device_id={"z": z_at(i)}, device_id_type=MESH)

    @pl.loop(1, NT)
    def _(i):
        pl.semaphore_signal(barrier, inc=1, device_id=to_tensor(tensor_at(i)), device_id_type=MESH)

    pl.semaphore_signal(barrier, inc=1, device_id=pair, device_id_type=MESH)
    pl.semaphore_signal(barrier, inc=1, device_id=core, device_id_type=MESH)

    @pl.when(off_diag)
    def _():
        pl.semaphore_signal(barrier, inc=1, device_id=mirror, device_id_type=MESH)
        pl.semaphore_wait(barrier, NZ + NT + 1)

    @pl.when(z == t)
    def _():
        pl.semaphore_wait(barrier, NZ + NT)

    tok_send = rdma(tok_ref, x_all.at[z], xin_s, xin_r, mirror)
    tok_here = pltpu.make_async_copy(tok_ref, x_all.at[t], xin_r)
    x_in = rdma(x_all.at[t], x_all.at[t], xin_s, xin_r, mirror)
    gain_send = rdma(gain_ref, gain_z, gain_s, gain_r, mirror)
    gain_here = pltpu.make_async_copy(gain_ref, gain_z, gain_r)
    cot_part = cot_ref.at[0, :, pl.ds(pl.multiple_of(t * feats, 128), feats)]
    cot_send = rdma(cot_part, c_all.at[z], cotp_s, cotp_r, mirror)
    cot_here = pltpu.make_async_copy(cot_part, c_all.at[t], cotp_r)
    cot_in = rdma(c_all.at[t], c_all.at[t], cotp_s, cotp_r, mirror)

    @pl.when(off_diag & (section == 0))
    def _():
        tok_send.start()

    @pl.when((z == t) & (section == 0))
    def _():
        tok_here.start()

    @pl.when(off_diag)
    def _():
        gain_send.start()

    @pl.when(z == t)
    def _():
        gain_here.start()

    mine = pl.ds(pl.multiple_of(xl * half, 128), half)
    up_send = rdma(up_ref.at[0], up_pair.at[mine], up_s, up_r, pair)
    up_send.start()

    @pl.when(off_diag)
    def _():
        cot_send.start()

    @pl.when(z == t)
    def _():
        cot_here.start()

    down_send = rdma(down_ref.at[0], down_pair.at[xl], down_s, down_r, pair)
    down_send.start()
    up_pair[mine, :] = up_ref[0]
    down_pair[xl] = down_ref[0]

    gain_send.wait_recv()
    x_in.wait_recv()

    def spread(i):
        return rdma(x_all.at[t], x_all.at[t], ag_s.at[i], ag_r.at[t], to_tensor(tensor_at(i)))

    @pl.loop(1, NT)
    def _(i):
        spread(i).start()

    up_send.wait_recv()
    gain_f = gain_z[...].astype(F32)
    up_all = up_pair

    def part_copy(k):
        return rdma(part_out.at[k], part_in.at[z], rz_s.at[k], rz_r.at[z], {"z": k})

    def sq_copy(k):
        return rdma(sq_out.at[k], sq_in.at[z], sq_s.at[k], sq_r.at[z], {"z": k})

    @pl.loop(0, NT)
    def _(i):
        k = tensor_at(i)

        @pl.when(i > 0)
        def _():
            rdma(x_all.at[k], x_all.at[k], ag_s.at[i], ag_r.at[k], to_tensor(k)).wait_recv()

        x_f = x_all[k].astype(F32)
        sq = x_f * x_f
        sq_hi = sq.astype(BF16)
        sq_lo = (sq - sq_hi.astype(F32)).astype(BF16)
        ones = jnp.ones((8, feats), BF16)
        row_dims = (((1,), (1,)), ((), ()))
        sq_row = lax.dot_general(ones, sq_hi, row_dims, preferred_element_type=F32)
        sq_row = sq_row + lax.dot_general(ones, sq_lo, row_dims, preferred_element_type=F32)
        scaled = (x_f * gain_f).astype(BF16)
        part = jnp.dot(scaled, up_all[...], preferred_element_type=F32).astype(BF16)

        @pl.when(k == z)
        def _():
            part_in[k] = part
            sq_in[k] = sq_row

        @pl.when(k != z)
        def _():
            part_out[k] = part
            sq_out[k] = sq_row
            part_copy(k).start()
            sq_copy(k).start()

    cot_in.wait_recv()

    def cot_spread(i):
        return rdma(c_all.at[t], c_all.at[t], cg_s.at[i], cg_r.at[t], to_tensor(tensor_at(i)))

    @pl.loop(1, NT)
    def _(i):
        cot_spread(i).start()

    acc[...] = part_in[z].astype(F32)

    def add_square(i, total):
        k = z_at(i)
        rdma(part_out.at[k], part_in.at[k], rz_s.at[k], rz_r.at[k], {"z": k}).wait_recv()
        rdma(sq_out.at[k], sq_in.at[k], sq_s.at[k], sq_r.at[k], {"z": k}).wait_recv()
        acc[...] += part_in[k].astype(F32)
        return total + sq_in[k]

    sq_sum = lax.fori_loop(1, NZ, add_square, sq_in[z])
    tokens = acc.shape[0]
    mean_col = jnp.transpose(jnp.broadcast_to(sq_sum[0:1, :], (tokens, tokens)))[:, 0:1] / width
    pre_act = acc[...] * lax.rsqrt(mean_col + EPS)
    hid_all[z] = jax.nn.gelu(pre_act, approximate=True).astype(BF16)

    def hid_spread(i):
        return rdma(hid_all.at[z], hid_all.at[z], az_s.at[i], az_r.at[z], {"z": z_at(i)})

    @pl.loop(1, NZ)
    def _(i):
        hid_spread(i).start()

    down_send.wait_recv()

    def y_copy(k):
        return rdma(y_out.at[k], y_in.at[t], rt_s.at[k], rt_r.at[t], to_tensor(k))

    @pl.loop(0, NZ)
    def _(i):
        k = z_at(i)

        @pl.when(i > 0)
        def _():
            rdma(hid_all.at[k], hid_all.at[k], az_s.at[i], az_r.at[k], {"z": k}).wait_recv()

        hid = hid_all[k]
        y_lo = jnp.dot(hid, down_pair[0], preferred_element_type=F32).astype(BF16)
        y_hi = jnp.dot(hid, down_pair[1], preferred_element_type=F32).astype(BF16)

        @pl.when(k == t)
        def _():
            y_in[k, :, 0:half] = y_lo
            y_in[k, :, half:] = y_hi

        @pl.when(k != t)
        def _():
            y_out[k, :, 0:half] = y_lo
            y_out[k, :, half:] = y_hi
            y_copy(k).start()

    @pl.loop(1, NT)
    def _(i):
        k = tensor_at(i)
        rdma(c_all.at[k], c_all.at[k], cg_s.at[i], cg_r.at[k], to_tensor(k)).wait_recv()

    hid_t = hid_all[...].reshape(NZ * tokens, hid_all.shape[2])

    def grad_half(which):
        cols = pl.ds(pl.multiple_of(which * half, 128), half)
        cot = c_all[:, :, cols].reshape(NZ * tokens, half)
        return lax.dot_general(hid_t, cot, (((0,), (0,)), ((), ())), preferred_element_type=F32)

    grad_out[...] = grad_half(1 - xl).astype(BF16)
    grad_send = rdma(grad_out, grad_in, gr_s, gr_r, pair)
    grad_send.start()
    grad_own[...] = grad_half(xl)

    acc_y = x_all[t].astype(F32) + y_in[t].astype(F32)

    def add_y(i, total):
        k = tensor_at(i)
        rdma(y_out.at[k], y_in.at[k], rt_s.at[k], rt_r.at[k], to_tensor(k)).wait_recv()
        return total + y_in[k].astype(F32)

    x_next[...] = lax.fori_loop(1, NT, add_y, acc_y).astype(BF16)

    core_send = rdma(x_next, x_all.at[t], core_s, xin_r, core)
    state_send = rdma(x_next, state_ref.at[0], out_s, out_r, mirror)
    state_here = pltpu.make_async_copy(x_next, state_ref.at[0], out_r)

    @pl.when(section == 0)
    def _():
        core_send.start()

    @pl.when(off_diag)
    def _():
        state_send.start()

    @pl.when(z == t)
    def _():
        state_here.start()

    grad_send.wait_recv()
    grad_ref[0] = (grad_own[...] + grad_in[...].astype(F32)).astype(BF16)

    @pl.when(section == 0)
    def _():
        core_send.wait_send()

    @pl.when(off_diag & (section == 0))
    def _():
        tok_send.wait_send()

    @pl.when(off_diag)
    def _():
        gain_send.wait_send()
        cot_send.wait_send()
        state_send.wait_send()

    up_send.wait_send()
    down_send.wait_send()
    grad_send.wait_send()

    @pl.loop(1, NT)
    def _(i):
        spread(i).wait_send()
        cot_spread(i).wait_send()
        y_copy(tensor_at(i)).wait_send()

    @pl.loop(1, NZ)
    def _(i):
        part_copy(z_at(i)).wait_send()
        sq_copy(z_at(i)).wait_send()
        hid_spread(i).wait_send()

    state_send.wait_recv()


def body(tokens, gain, w_up, w_down, cotangent):
    rows, feats = tokens.shape
    half, hidden = w_up.shape[1:]
    width = cotangent.shape[2]
    dma = pltpu.SemaphoreType.DMA
    vmem = pl.BlockSpec(memory_space=pltpu.VMEM)

    def run(*refs):
        kernel(width, *refs)

    one = dma(())
    states, grads = pl.pallas_call(
        run,
        out_shape=(
            jax.ShapeDtypeStruct((1, rows, feats), BF16),
            jax.ShapeDtypeStruct((1, hidden, half), BF16),
        ),
        in_specs=[vmem] * 5,
        out_specs=(vmem, vmem),
        scratch_shapes=[
            pltpu.VMEM((NT, rows, feats), BF16),
            pltpu.VMEM((NT, rows, feats), BF16),
            pltpu.VMEM((1, feats), BF16),
            pltpu.VMEM((2 * half, hidden), BF16),
            pltpu.VMEM((2, hidden, half), BF16),
            pltpu.VMEM((NZ, rows, hidden), BF16),
            pltpu.VMEM((NZ, rows, hidden), BF16),
            pltpu.VMEM((NZ, 8, rows), F32),
            pltpu.VMEM((NZ, 8, rows), F32),
            pltpu.VMEM((rows, hidden), F32),
            pltpu.VMEM((NZ, rows, hidden), BF16),
            pltpu.VMEM((NT, rows, feats), BF16),
            pltpu.VMEM((NT, rows, feats), BF16),
            pltpu.VMEM((rows, feats), BF16),
            pltpu.VMEM((hidden, half), F32),
            pltpu.VMEM((hidden, half), BF16),
            pltpu.VMEM((hidden, half), BF16),
        ]
        + [one] * 11
        + [dma((8,))] * 12
        + [one] * 4,
        compiler_params=pltpu.CompilerParams(
            collective_id=0, has_side_effects=True, vmem_limit_bytes=48 * 1024 * 1024
        ),
    )(tokens, gain, w_up, w_down, cotangent)
    return states, grads


def solution(mesh):
    torus = Mesh(
        mesh.devices.reshape(mesh.shape["section"], NZ, 2, NY, NX),
        ("section", "z", "xl", "y", "xh"),
    )
    dp, tensor = ("z", "xl"), ("y", "xh")
    in_specs = (
        P(dp, tensor),
        P("section", tensor),
        P("section", dp, tensor),
        P("section", tensor, dp),
        P("section", dp, None),
    )
    out_specs = (P("section", dp, tensor), P("section", tensor, dp))
    return jax.shard_map(body, mesh=torus, in_specs=in_specs, out_specs=out_specs, check_vma=False)
```

time: 378 us -> 151 us (0.40); the launches traced: 372 us -> 151 us
  waiting for transfers between devices: 201 us -> 0 us
  Pallas kernels: 0 us -> 144 us
  blocking collectives: 91.1 us -> 0 us
  starting transfers between devices: 27.9 us -> 0 us
  matrix products: 16.4 us -> 0 us
  between operations: 14 us -> 0.65 us
  local copies, waits for them, and re-layouts: 16.2 us -> 6.13 us
  other arithmetic: 5.32 us -> 0 us
    pallas_call x0 -> x1, Pallas kernels: none -> 144 us  [body(): pl.pallas_call(run, out_shape=(jax.ShapeDtypeStruct((1, rows, feats), BF1...]
    all_gather x3 -> x0, waiting for transfers between devices: 129 us -> none  [the longest x2 96.5 us: gathered_by_axis(): filled = lax.all_gather(filled, axes[number], axis=dim, tiled=True)]
    all_to_all x6 -> x0, waiting for transfers between devices: 61.7 us -> none  [the longest x3 32.7 us: copy_for_each(): lax.all_to_all(jnp.broadcast_to(array[None], (peers, *array.shape)), axis...]
    all_gather x3 -> x0, blocking collectives: 48.2 us -> none  [the longest x1 28.3 us: body(): gain_whole = lax.all_gather(gain_own, 'tensor', axis=0, tiled=True)]
    all_to_all x1 -> x0, blocking collectives: 42.9 us -> none  [body(): lax.all_to_all(cot_own, DP, split_axis=1, concat_axis=0, tiled=True)]
    all_to_all x6 -> x0, starting transfers between devices: 23.9 us -> none  [the longest x3 13.4 us: copy_for_each(): lax.all_to_all(jnp.broadcast_to(array[None], (peers, *array.shape)), axis...]
    dot_general x20 -> x0, matrix products: 16.4 us -> none  [the longest x16 9.16 us: body(): lax.dot_general(hidden_all[lower:lower + tok_rows], cot_mine[lower:lower...]
    ppermute x3 -> x0, waiting for transfers between devices: 10.6 us -> none  [shifted(): return lax.ppermute(array, axis, pairs)]
  transfers between devices with their start and end apart: 12 -> 0, of which waited for: 12 -> 0; matrix products, arithmetic and copies ran while one was open for 1% -> 0% of each run, Pallas kernels for 0% -> 0%
where the time goes in v1:
time: 151 us
  Pallas kernels  144 us (95%)
  local copies, waits for them, and re-layouts  6.13 us (4%)
    pallas_call x1, Pallas kernels, body(): pl.pallas_call(run, out_shape=(jax.ShapeDtypeStruct((1, rows, feats), BF1...  144 us
    unnamed x12, local copies, waits for them, and re-layouts  6.13 us

profile of v1, /device:TPU:1, one launch (start us, length us, event | category | flops | bytes accessed | tf_op | source)
XLA Modules:
  0.0 150.8 jit_solution(7108226081332980488)
XLA Ops:
  0.6 0.0 copy-start
  0.6 1.2 copy-done
  1.9 0.0 copy-start.1
  1.9 1.0 copy-done.1
  2.8 0.0 copy-start.2
  2.8 1.0 copy-done.2
  3.8 0.0 copy-start.3
  3.8 0.9 copy-done.3
  4.7 0.0 copy-start.4
  4.7 0.7 copy-done.4
  5.4 144.0 %shard_map.68 = (bf16[1,128,512]{2,1,0:T(8,128)(2,1)S(1)}, bf16[1,640,256]{2,1,0:T(8,128)(2,1)S(1)}) custom-call(bf16[128,512]{1,0:T(8,128)(2,1)S(1)} %copy-done.3, bf16[1,512]{1,0:T(2,128)(2,1)S(1)} %copy-done.4, bf16[1,256,640]{2,1,0:T(8,128)(2,1)S(1)} %copy-done.1, bf16[1,640,256]{2,1,0:T(8,128)(2,1)S(1)} %copy-done.2, bf16[1,128,4096]{2,1,0:T(8,128)(2,1)S(1)} %copy-done), custom_call_target="tpu_custom_call" | custom-call | tf_op jit(solution)/shard_map/pallas_call | solution.py:325
  149.4 0.7 copy.9
  150.1 0.7 copy.10
Async XLA Ops:
  0.6 1.2 copy-start
  1.9 1.0 copy-start.1
  2.8 1.0 copy-start.2
  3.8 0.9 copy-start.3
  4.7 0.7 copy-start.4

commit v2 on v1

v2 whole, which is shorter than its diff:
```python
import jax
import jax.numpy as jnp
from jax import lax
from jax.experimental import pallas as pl
from jax.experimental.pallas import tpu as pltpu
from jax.sharding import Mesh
from jax.sharding import PartitionSpec as P

EPS = 1e-06
MESH = pl.DeviceIdType.MESH
NZ, NY, NX = 8, 4, 2
NT = NY * NX
PARTS = 2
F32, BF16 = jnp.float32, jnp.bfloat16


def ring_offset(i):
    return ((i + 1) // 2) * (1 - 2 * ((i + 1) % 2))


def kernel(
    width,
    tok_ref, gain_ref, up_ref, down_ref, cot_ref,
    state_ref, grad_ref,
    x_all, c_all, gain_z, up_pair, down_pair,
    part_out, part_in, sq_out, sq_in, acc, hid_all, y_out, y_in, x_next,
    grad_own, grad_out, grad_in, grad_done,
    gain_s, gain_r, cotp_s, cotp_r, up_s, up_r, down_s, down_r, upl, downl,
    gr_s, gr_r, gd_s, cg_s, cg_r,
    xin_s, xin_r, core_s, out_s, out_r,
    ag_s, ag_r, rz_s, rz_r, sq_s, sq_r, az_s, az_r, rt_s, rt_r,
    go,
):
    section = lax.axis_index("section")
    z = lax.axis_index("z")
    xl = lax.axis_index("xl")
    y = lax.axis_index("y")
    xh = lax.axis_index("xh")
    t = y * NX + xh
    half = up_ref.shape[1]
    feats = tok_ref.shape[1]
    tokens = tok_ref.shape[0]
    rows = tokens // PARTS
    hidden = up_ref.shape[2]
    pair = {"xl": 1 - xl}
    core = {"section": 1 - section}
    mirror = {"z": t, "y": z // NX, "xh": z % NX}
    off_diag = z != t

    def to_tensor(k):
        return {"y": k // NX, "xh": k % NX}

    def tensor_at(i):
        k = i % NY
        step = k + (k // 2) * (1 - 2 * (k % 2))
        return ((y + step) % NY) * NX + (xh + i // NY) % NX

    def z_at(i):
        return (z + ring_offset(i) + NZ) % NZ

    def part(m):
        return pl.ds(m * rows, rows)

    def rdma(src, dst, ssem, rsem, dev):
        return pltpu.make_async_remote_copy(
            src_ref=src, dst_ref=dst, send_sem=ssem, recv_sem=rsem,
            device_id=dev, device_id_type=MESH,
        )

    with jax.named_scope("barrier"):
        mine = pl.ds(pl.multiple_of(xl * half, 128), half)
        up_here = pltpu.make_async_copy(up_ref.at[0], up_pair.at[mine], upl)
        down_here = pltpu.make_async_copy(down_ref.at[0], down_pair.at[xl], downl)
        up_here.start()
        down_here.start()
        barrier = pltpu.get_barrier_semaphore()

        @pl.loop(1, NZ)
        def _(i):
            pl.semaphore_signal(barrier, inc=1, device_id={"z": z_at(i)}, device_id_type=MESH)

        @pl.loop(1, NT)
        def _(i):
            pl.semaphore_signal(
                barrier, inc=1, device_id=to_tensor(tensor_at(i)), device_id_type=MESH
            )

        pl.semaphore_signal(barrier, inc=1, device_id=pair, device_id_type=MESH)
        pl.semaphore_signal(barrier, inc=1, device_id=core, device_id_type=MESH)

        @pl.when(off_diag)
        def _():
            pl.semaphore_signal(barrier, inc=1, device_id=mirror, device_id_type=MESH)
            pl.semaphore_wait(barrier, NZ + NT + 1)

        @pl.when(z == t)
        def _():
            pl.semaphore_wait(barrier, NZ + NT)

    def tok_send(m):
        return rdma(tok_ref.at[part(m)], x_all.at[z, part(m)], xin_s.at[m], xin_r.at[m], mirror)

    def tok_here(m):
        return pltpu.make_async_copy(tok_ref.at[part(m)], x_all.at[t, part(m)], xin_r.at[m])

    def x_in(m):
        return rdma(x_all.at[t, part(m)], x_all.at[t, part(m)], xin_s.at[m], xin_r.at[m], mirror)

    gain_send = rdma(gain_ref, gain_z, gain_s, gain_r, mirror)
    gain_here = pltpu.make_async_copy(gain_ref, gain_z, gain_r)
    cot_part = cot_ref.at[0, :, pl.ds(pl.multiple_of(t * feats, 128), feats)]
    cot_send = rdma(cot_part, c_all.at[z], cotp_s, cotp_r, mirror)
    cot_here = pltpu.make_async_copy(cot_part, c_all.at[t], cotp_r)
    cot_in = rdma(c_all.at[t], c_all.at[t], cotp_s, cotp_r, mirror)
    up_send = rdma(up_ref.at[0], up_pair.at[mine], up_s, up_r, pair)
    down_send = rdma(down_ref.at[0], down_pair.at[xl], down_s, down_r, pair)

    def start_cot():
        @pl.when(off_diag)
        def _():
            cot_send.start()

        @pl.when(z == t)
        def _():
            cot_here.start()

    def go_on():
        pl.semaphore_signal(go, inc=1, device_id=core, device_id_type=MESH)

    with jax.named_scope("send0"):
        @pl.when(off_diag & (section == 0))
        def _():
            for m in range(PARTS):
                tok_send(m).start()

        @pl.when((z == t) & (section == 0))
        def _():
            for m in range(PARTS):
                tok_here(m).start()

        @pl.when(off_diag)
        def _():
            gain_send.start()

        @pl.when(z == t)
        def _():
            gain_here.start()

    with jax.named_scope("background"):
        @pl.when(section == 0)
        def _():
            up_send.start()

        @pl.when(section == 1)
        def _():
            pl.semaphore_wait(go, 1)
            start_cot()
            pl.semaphore_wait(go, 1)
            up_send.start()
            down_send.start()

    def spread(m, i):
        return rdma(
            x_all.at[t, part(m)], x_all.at[t, part(m)],
            ag_s.at[m * NT + i], ag_r.at[m * NT + t], to_tensor(tensor_at(i)),
        )

    def take_x(m):
        x_in(m).wait_recv()

        @pl.loop(1, NT)
        def _(i):
            spread(m, i).start()

    with jax.named_scope("waitx"):
        take_x(0)

        @pl.when(section == 0)
        def _():
            for m in range(1, PARTS):
                take_x(m)
            go_on()
            start_cot()

    with jax.named_scope("waitup"):
        gain_send.wait_recv()
        up_here.wait()
        up_send.wait_recv()

    def part_copy(m, k):
        return rdma(
            part_out.at[k, part(m)], part_in.at[z, part(m)],
            rz_s.at[m * NZ + k], rz_r.at[m * NZ + z], {"z": k},
        )

    def sq_copy(m, k):
        return rdma(
            sq_out.at[m, k], sq_in.at[m, z], sq_s.at[m * NZ + k], sq_r.at[m * NZ + z], {"z": k}
        )

    def up_stage(m):
        gain_f = gain_z[...].astype(F32)

        @pl.loop(0, NT)
        def _(i):
            k = tensor_at(i)

            @pl.when(i > 0)
            def _():
                rdma(
                    x_all.at[k, part(m)], x_all.at[k, part(m)],
                    ag_s.at[m * NT + i], ag_r.at[m * NT + k], to_tensor(k),
                ).wait_recv()

            x_f = x_all[k, m * rows:(m + 1) * rows].astype(F32)
            sq = jnp.concatenate([x_f * x_f] * PARTS, axis=0)
            sq_hi = sq.astype(BF16)
            sq_lo = (sq - sq_hi.astype(F32)).astype(BF16)
            ones = jnp.ones((8, feats), BF16)
            row_dims = (((1,), (1,)), ((), ()))
            sq_row = lax.dot_general(ones, sq_hi, row_dims, preferred_element_type=F32)
            sq_row = sq_row + lax.dot_general(ones, sq_lo, row_dims, preferred_element_type=F32)
            scaled = (x_f * gain_f).astype(BF16)
            value = jnp.dot(scaled, up_pair[...], preferred_element_type=F32).astype(BF16)

            @pl.when(k == z)
            def _():
                part_in[k, m * rows:(m + 1) * rows] = value
                sq_in[m, k] = sq_row

            @pl.when(k != z)
            def _():
                part_out[k, m * rows:(m + 1) * rows] = value
                sq_out[m, k] = sq_row
                part_copy(m, k).start()
                sq_copy(m, k).start()

    def hid_spread(m, i):
        return rdma(
            hid_all.at[z, part(m)], hid_all.at[z, part(m)],
            az_s.at[m * NZ + i], az_r.at[m * NZ + z], {"z": z_at(i)},
        )

    def hid_stage(m):
        acc[...] = part_in[z, m * rows:(m + 1) * rows].astype(F32)

        def add_square(i, total):
            k = z_at(i)
            rdma(
                part_out.at[k, part(m)], part_in.at[k, part(m)],
                rz_s.at[m * NZ + k], rz_r.at[m * NZ + k], {"z": k},
            ).wait_recv()
            rdma(
                sq_out.at[m, k], sq_in.at[m, k],
                sq_s.at[m * NZ + k], sq_r.at[m * NZ + k], {"z": k},
            ).wait_recv()
            acc[...] += part_in[k, m * rows:(m + 1) * rows].astype(F32)
            return total + sq_in[m, k]

        sq_sum = lax.fori_loop(1, NZ, add_square, sq_in[m, z])
        square = jnp.transpose(jnp.broadcast_to(sq_sum[0:1, :], (tokens, tokens)))
        mean_col = square[0:rows, 0:1] / width
        pre_act = acc[...] * lax.rsqrt(mean_col + EPS)
        hid_all[z, m * rows:(m + 1) * rows] = jax.nn.gelu(pre_act, approximate=True).astype(BF16)

        @pl.loop(1, NZ)
        def _(i):
            hid_spread(m, i).start()

    def y_copy(m, k):
        return rdma(
            y_out.at[k, part(m)], y_in.at[t, part(m)],
            rt_s.at[m * NT + k], rt_r.at[m * NT + t], to_tensor(k),
        )

    def down_stage(m):
        @pl.loop(0, NZ)
        def _(i):
            k = z_at(i)

            @pl.when(i > 0)
            def _():
                rdma(
                    hid_all.at[k, part(m)], hid_all.at[k, part(m)],
                    az_s.at[m * NZ + i], az_r.at[m * NZ + k], {"z": k},
                ).wait_recv()

            hid = hid_all[k, m * rows:(m + 1) * rows]
            y_lo = jnp.dot(hid, down_pair[0], preferred_element_type=F32).astype(BF16)
            y_hi = jnp.dot(hid, down_pair[1], preferred_element_type=F32).astype(BF16)

            @pl.when(k == t)
            def _():
                y_in[k, m * rows:(m + 1) * rows, 0:half] = y_lo
                y_in[k, m * rows:(m + 1) * rows, half:] = y_hi

            @pl.when(k != t)
            def _():
                y_out[k, m * rows:(m + 1) * rows, 0:half] = y_lo
                y_out[k, m * rows:(m + 1) * rows, half:] = y_hi
                y_copy(m, k).start()

    def core_send(m):
        return rdma(x_next.at[part(m)], x_all.at[t, part(m)], core_s.at[m], xin_r.at[m], core)

    def state_send(m):
        return rdma(x_next.at[part(m)], state_ref.at[0, part(m)], out_s.at[m], out_r.at[m], mirror)

    def state_here(m):
        return pltpu.make_async_copy(x_next.at[part(m)], state_ref.at[0, part(m)], out_r.at[m])

    def next_stage(m):
        def add_y(i, total):
            k = tensor_at(i)
            rdma(
                y_out.at[k, part(m)], y_in.at[k, part(m)],
                rt_s.at[m * NT + k], rt_r.at[m * NT + k], to_tensor(k),
            ).wait_recv()
            return total + y_in[k, m * rows:(m + 1) * rows].astype(F32)

        first = x_all[t, m * rows:(m + 1) * rows].astype(F32)
        first = first + y_in[t, m * rows:(m + 1) * rows].astype(F32)
        x_next[m * rows:(m + 1) * rows] = lax.fori_loop(1, NT, add_y, first).astype(BF16)

        @pl.when(section == 0)
        def _():
            core_send(m).start()

        @pl.when(off_diag)
        def _():
            state_send(m).start()

        @pl.when(z == t)
        def _():
            state_here(m).start()

    def cot_spread(i):
        return rdma(c_all.at[t], c_all.at[t], cg_s.at[i], cg_r.at[t], to_tensor(tensor_at(i)))

    for m in range(PARTS):
        if m > 0:
            with jax.named_scope("waitx%d" % m):
                @pl.when(section == 1)
                def _():
                    take_x(m)
        with jax.named_scope("up%d" % m):
            up_stage(m)

    with jax.named_scope("waitcot"):
        @pl.when(section == 0)
        def _():
            down_send.start()
            go_on()

        cot_in.wait_recv()

        @pl.loop(1, NT)
        def _(i):
            cot_spread(i).start()

    for m in range(PARTS):
        with jax.named_scope("hid%d" % m):
            hid_stage(m)

    with jax.named_scope("waitdown"):
        down_here.wait()
        down_send.wait_recv()

    for m in range(PARTS - 1):
        with jax.named_scope("down%d" % m):
            down_stage(m)
        with jax.named_scope("next%d" % m):
            next_stage(m)
    with jax.named_scope("down%d" % (PARTS - 1)):
        down_stage(PARTS - 1)

    with jax.named_scope("waitcg"):
        @pl.loop(1, NT)
        def _(i):
            k = tensor_at(i)
            rdma(c_all.at[k], c_all.at[k], cg_s.at[i], cg_r.at[k], to_tensor(k)).wait_recv()

    def grad_half(which):
        hid_t = hid_all[...].reshape(NZ * tokens, hidden)
        cols = pl.ds(pl.multiple_of(which * half, 128), half)
        cot = c_all[:, :, cols].reshape(NZ * tokens, half)
        return lax.dot_general(hid_t, cot, (((0,), (0,)), ((), ())), preferred_element_type=F32)

    grad_send = rdma(grad_out, grad_in, gr_s, gr_r, pair)

    def grad_stage():
        grad_out[...] = grad_half(1 - xl).astype(BF16)
        grad_send.start()
        grad_own[...] = grad_half(xl)

    with jax.named_scope("grad1"):
        @pl.when(section == 1)
        def _():
            grad_stage()

    with jax.named_scope("next%d" % (PARTS - 1)):
        next_stage(PARTS - 1)

    with jax.named_scope("grad0"):
        @pl.when(section == 0)
        def _():
            grad_stage()

    with jax.named_scope("waitgrad"):
        grad_send.wait_recv()
        grad_done[...] = (grad_own[...] + grad_in[...].astype(F32)).astype(BF16)
        grad_store = pltpu.make_async_copy(grad_done, grad_ref.at[0], gd_s)
        grad_store.start()

    with jax.named_scope("drain"):
        @pl.when(section == 0)
        def _():
            for m in range(PARTS):
                core_send(m).wait_send()

        @pl.when(off_diag & (section == 0))
        def _():
            for m in range(PARTS):
                tok_send(m).wait_send()

        @pl.when(off_diag)
        def _():
            gain_send.wait_send()
            cot_send.wait_send()
            for m in range(PARTS):
                state_send(m).wait_send()

        up_send.wait_send()
        down_send.wait_send()
        grad_send.wait_send()

        @pl.loop(1, NT)
        def _(i):
            cot_spread(i).wait_send()
            for m in range(PARTS):
                spread(m, i).wait_send()
                y_copy(m, tensor_at(i)).wait_send()

        @pl.loop(1, NZ)
        def _(i):
            for m in range(PARTS):
                part_copy(m, z_at(i)).wait_send()
                sq_copy(m, z_at(i)).wait_send()
                hid_spread(m, i).wait_send()

    with jax.named_scope("waitstate"):
        for m in range(PARTS):
            state_send(m).wait_recv()
        grad_store.wait()


def body(tokens, gain, w_up, w_down, cotangent):
    rows, feats = tokens.shape
    half, hidden = w_up.shape[1:]
    width = cotangent.shape[2]
    dma = pltpu.SemaphoreType.DMA
    vmem = pl.BlockSpec(memory_space=pltpu.VMEM)
    hbm = pl.BlockSpec(memory_space=pl.ANY)

    def run(*refs):
        kernel(width, *refs)

    one = dma(())
    states, grads = pl.pallas_call(
        run,
        out_shape=(
            jax.ShapeDtypeStruct((1, rows, feats), BF16),
            jax.ShapeDtypeStruct((1, hidden, half), BF16),
        ),
        in_specs=[hbm] * 5,
        out_specs=(hbm, hbm),
        scratch_shapes=[
            pltpu.VMEM((NT, rows, feats), BF16),
            pltpu.VMEM((NT, rows, feats), BF16),
            pltpu.VMEM((1, feats), BF16),
            pltpu.VMEM((2 * half, hidden), BF16),
            pltpu.VMEM((2, hidden, half), BF16),
            pltpu.VMEM((NZ, rows, hidden), BF16),
            pltpu.VMEM((NZ, rows, hidden), BF16),
            pltpu.VMEM((PARTS, NZ, 8, rows), F32),
            pltpu.VMEM((PARTS, NZ, 8, rows), F32),
            pltpu.VMEM((rows // PARTS, hidden), F32),
            pltpu.VMEM((NZ, rows, hidden), BF16),
            pltpu.VMEM((NT, rows, feats), BF16),
            pltpu.VMEM((NT, rows, feats), BF16),
            pltpu.VMEM((rows, feats), BF16),
            pltpu.VMEM((hidden, half), F32),
            pltpu.VMEM((hidden, half), BF16),
            pltpu.VMEM((hidden, half), BF16),
            pltpu.VMEM((hidden, half), BF16),
        ]
        + [one] * 13
        + [dma((8,))] * 2
        + [dma((PARTS,))] * 5
        + [dma((8 * PARTS,))] * 10
        + [pltpu.SemaphoreType.REGULAR],
        compiler_params=pltpu.CompilerParams(
            collective_id=0, has_side_effects=True, vmem_limit_bytes=60 * 1024 * 1024
        ),
    )(tokens, gain, w_up, w_down, cotangent)
    return states, grads


def solution(mesh):
    torus = Mesh(
        mesh.devices.reshape(mesh.shape["section"], NZ, 2, NY, NX),
        ("section", "z", "xl", "y", "xh"),
    )
    dp, tensor = ("z", "xl"), ("y", "xh")
    in_specs = (
        P(dp, tensor),
        P("section", tensor),
        P("section", dp, tensor),
        P("section", tensor, dp),
        P("section", dp, None),
    )
    out_specs = (P("section", dp, tensor), P("section", tensor, dp))
    return jax.shard_map(body, mesh=torus, in_specs=in_specs, out_specs=out_specs, check_vma=False)
```

time: 151 us -> 125 us (0.83)
  the two profiles are of different devices: /device:TPU:1 before, /device:TPU:7 now
where the time goes in v2:
time: 125 us
  Pallas kernels  121 us (97%)
  local copies, waits for them, and re-layouts  3.29 us (3%)
    pallas_call x1, Pallas kernels, body(): pl.pallas_call(run, out_shape=(jax.ShapeDtypeStruct((1, rows, feats), BF1...  121 us
    unnamed x2, local copies, waits for them, and re-layouts  3.29 us

profile of v2, /device:TPU:7, one launch (start us, length us, event | category | flops | bytes accessed | tf_op | source)
XLA Modules:
  0.0 124.6 jit_solution(10087618632631914987)
XLA Ops:
  0.6 120.7 %shard_map.68 = (bf16[1,128,512]{2,1,0:T(8,128)(2,1)}, bf16[1,640,256]{2,1,0:T(8,128)(2,1)}) custom-call(bf16[128,512]{1,0:T(8,128)(2,1)} %refs_0_.1, bf16[1,512]{1,0:T(2,128)(2,1)} %refs_1_.1, bf16[1,256,640]{2,1,0:T(8,128)(2,1)} %refs_2_.1, bf16[1,640,256]{2,1,0:T(8,128)(2,1)} %refs_3_.1, bf16[1,128,4096]{2,1,0:T(8,128)(2,1)} %refs_4_.1), custom_call_target="tpu_custom_call" | custom-call | tf_op jit(solution)/shard_map/pallas_call | solution.py:469
  121.3 1.6 %copy.9 = bf16[1,128,512]{2,1,0:T(8,128)(2,1)} copy(bf16[1,128,512]{2,1,0:T(8,128)(2,1)} %get-tuple-element.4) | data formatting | bytes 262144
  122.9 1.7 %copy.10 = bf16[1,640,256]{2,1,0:T(8,128)(2,1)} copy(bf16[1,640,256]{2,1,0:T(8,128)(2,1)} %get-tuple-element.5) | data formatting | bytes 655360

commit v3 on v2

--- a/solution.py
+++ b/solution.py
@@ -26,7 +26,7 @@
     part_out, part_in, sq_out, sq_in, acc, hid_all, y_out, y_in, x_next,
     grad_own, grad_out, grad_in, grad_done,
     gain_s, gain_r, cotp_s, cotp_r, up_s, up_r, down_s, down_r, upl, downl,
-    gr_s, gr_r, gd_s, cg_s, cg_r,
+    gr_s, gr_r, gd_s, cotl, cg_s, cg_r,
     xin_s, xin_r, core_s, out_s, out_r,
     ag_s, ag_r, rz_s, rz_r, sq_s, sq_r, az_s, az_r, rt_s, rt_r,
     go,
@@ -44,8 +44,12 @@
     hidden = up_ref.shape[2]
     pair = {"xl": 1 - xl}
     core = {"section": 1 - section}
-    mirror = {"z": t, "y": z // NX, "xh": z % NX}
-    off_diag = z != t
+    own = (t - z + NT) % NT
+    ahead_t = (z + t) % NT
+    ahead = {"z": t, "y": ahead_t // NX, "xh": ahead_t % NX}
+    back = {"z": own, "y": z // NX, "xh": z % NX}
+    moves = (z + t) > 0
+    shares_cot = own != z
 
     def to_tensor(k):
         return {"y": k // NX, "xh": k % NX}
@@ -54,6 +58,9 @@
         k = i % NY
         step = k + (k // 2) * (1 - 2 * (k % 2))
         return ((y + step) % NY) * NX + (xh + i // NY) % NX
+
+    def block_at(i):
+        return (tensor_at(i) - z + NT) % NT
 
     def z_at(i):
         return (z + ring_offset(i) + NZ) % NZ
@@ -88,63 +95,79 @@
         pl.semaphore_signal(barrier, inc=1, device_id=pair, device_id_type=MESH)
         pl.semaphore_signal(barrier, inc=1, device_id=core, device_id_type=MESH)
 
-        @pl.when(off_diag)
-        def _():
-            pl.semaphore_signal(barrier, inc=1, device_id=mirror, device_id_type=MESH)
-            pl.semaphore_wait(barrier, NZ + NT + 1)
-
-        @pl.when(z == t)
+        @pl.when(moves)
+        def _():
+            pl.semaphore_signal(barrier, inc=1, device_id=ahead, device_id_type=MESH)
+            pl.semaphore_signal(barrier, inc=1, device_id=back, device_id_type=MESH)
+            pl.semaphore_wait(barrier, NZ + NT + 2)
+
+        @pl.when(z + t == 0)
         def _():
             pl.semaphore_wait(barrier, NZ + NT)
 
     def tok_send(m):
-        return rdma(tok_ref.at[part(m)], x_all.at[z, part(m)], xin_s.at[m], xin_r.at[m], mirror)
+        return rdma(tok_ref.at[part(m)], x_all.at[z, part(m)], xin_s.at[m], xin_r.at[m], ahead)
 
     def tok_here(m):
-        return pltpu.make_async_copy(tok_ref.at[part(m)], x_all.at[t, part(m)], xin_r.at[m])
+        return pltpu.make_async_copy(tok_ref.at[part(m)], x_all.at[own, part(m)], xin_r.at[m])
 
     def x_in(m):
-        return rdma(x_all.at[t, part(m)], x_all.at[t, part(m)], xin_s.at[m], xin_r.at[m], mirror)
-
-    gain_send = rdma(gain_ref, gain_z, gain_s, gain_r, mirror)
+        return rdma(x_all.at[own, part(m)], x_all.at[own, part(m)], xin_s.at[m], xin_r.at[m], back)
+
+    gain_send = rdma(gain_ref, gain_z, gain_s, gain_r, ahead)
     gain_here = pltpu.make_async_copy(gain_ref, gain_z, gain_r)
-    cot_part = cot_ref.at[0, :, pl.ds(pl.multiple_of(t * feats, 128), feats)]
-    cot_send = rdma(cot_part, c_all.at[z], cotp_s, cotp_r, mirror)
-    cot_here = pltpu.make_async_copy(cot_part, c_all.at[t], cotp_r)
-    cot_in = rdma(c_all.at[t], c_all.at[t], cotp_s, cotp_r, mirror)
+
+    def cot_cols(k):
+        return cot_ref.at[0, :, pl.ds(pl.multiple_of(k * feats, 128), feats)]
+
+    cot_send = rdma(cot_cols(own), c_all.at[z], cotp_s, cotp_r, {"z": own})
+    cot_in = rdma(c_all.at[own], c_all.at[own], cotp_s, cotp_r, {"z": own})
+    cot_here = pltpu.make_async_copy(cot_cols(z), c_all.at[z], cotl)
     up_send = rdma(up_ref.at[0], up_pair.at[mine], up_s, up_r, pair)
     down_send = rdma(down_ref.at[0], down_pair.at[xl], down_s, down_r, pair)
 
     def start_cot():
-        @pl.when(off_diag)
+        @pl.when(shares_cot)
         def _():
             cot_send.start()
 
-        @pl.when(z == t)
-        def _():
-            cot_here.start()
+    def cot_spread(i):
+        return rdma(
+            c_all.at[own], c_all.at[own], cg_s.at[i], cg_r.at[own], to_tensor(tensor_at(i))
+        )
+
+    def spread_cot():
+        @pl.when(shares_cot)
+        def _():
+            cot_in.wait_recv()
+
+            @pl.loop(1, NT)
+            def _(i):
+                cot_spread(i).start()
 
     def go_on():
         pl.semaphore_signal(go, inc=1, device_id=core, device_id_type=MESH)
 
     with jax.named_scope("send0"):
-        @pl.when(off_diag & (section == 0))
+        @pl.when(moves & (section == 0))
         def _():
             for m in range(PARTS):
                 tok_send(m).start()
 
-        @pl.when((z == t) & (section == 0))
+        @pl.when((z + t == 0) & (section == 0))
         def _():
             for m in range(PARTS):
                 tok_here(m).start()
 
-        @pl.when(off_diag)
+        @pl.when(moves)
         def _():
             gain_send.start()
 
-        @pl.when(z == t)
+        @pl.when(z + t == 0)
         def _():
             gain_here.start()
+
+        cot_here.start()
 
     with jax.named_scope("background"):
         @pl.when(section == 0)
@@ -158,11 +181,12 @@
             pl.semaphore_wait(go, 1)
             up_send.start()
             down_send.start()
+            spread_cot()
 
     def spread(m, i):
         return rdma(
-            x_all.at[t, part(m)], x_all.at[t, part(m)],
-            ag_s.at[m * NT + i], ag_r.at[m * NT + t], to_tensor(tensor_at(i)),
+            x_all.at[own, part(m)], x_all.at[own, part(m)],
+            ag_s.at[m * NT + i], ag_r.at[m * NT + own], to_tensor(tensor_at(i)),
         )
 
     def take_x(m):
@@ -179,8 +203,8 @@
         def _():
             for m in range(1, PARTS):
                 take_x(m)
+            start_cot()
             go_on()
-            start_cot()
 
     with jax.named_scope("waitup"):
         gain_send.wait_recv()
@@ -203,13 +227,13 @@
 
         @pl.loop(0, NT)
         def _(i):
-            k = tensor_at(i)
+            k = block_at(i)
 
             @pl.when(i > 0)
             def _():
                 rdma(
                     x_all.at[k, part(m)], x_all.at[k, part(m)],
-                    ag_s.at[m * NT + i], ag_r.at[m * NT + k], to_tensor(k),
+                    ag_s.at[m * NT + i], ag_r.at[m * NT + k], to_tensor(tensor_at(i)),
                 ).wait_recv()
 
             x_f = x_all[k, m * rows:(m + 1) * rows].astype(F32)
@@ -270,11 +294,11 @@
     def y_copy(m, k):
         return rdma(
             y_out.at[k, part(m)], y_in.at[t, part(m)],
-            rt_s.at[m * NT + k], rt_r.at[m * NT + t], to_tensor(k),
-        )
-
-    def down_stage(m):
-        @pl.loop(0, NZ)
+            rt_s.at[m * NT + k], rt_r.at[m * NT + t], to_tensor((k + z) % NT),
+        )
+
+    def down_stage(m, first, last):
+        @pl.loop(first, last)
         def _(i):
             k = z_at(i)
 
@@ -289,22 +313,22 @@
             y_lo = jnp.dot(hid, down_pair[0], preferred_element_type=F32).astype(BF16)
             y_hi = jnp.dot(hid, down_pair[1], preferred_element_type=F32).astype(BF16)
 
-            @pl.when(k == t)
-            def _():
-                y_in[k, m * rows:(m + 1) * rows, 0:half] = y_lo
-                y_in[k, m * rows:(m + 1) * rows, half:] = y_hi
-
-            @pl.when(k != t)
+            @pl.when(k == own)
+            def _():
+                y_in[t, m * rows:(m + 1) * rows, 0:half] = y_lo
+                y_in[t, m * rows:(m + 1) * rows, half:] = y_hi
+
+            @pl.when(k != own)
             def _():
                 y_out[k, m * rows:(m + 1) * rows, 0:half] = y_lo
                 y_out[k, m * rows:(m + 1) * rows, half:] = y_hi
                 y_copy(m, k).start()
 
     def core_send(m):
-        return rdma(x_next.at[part(m)], x_all.at[t, part(m)], core_s.at[m], xin_r.at[m], core)
+        return rdma(x_next.at[part(m)], x_all.at[own, part(m)], core_s.at[m], xin_r.at[m], core)
 
     def state_send(m):
-        return rdma(x_next.at[part(m)], state_ref.at[0, part(m)], out_s.at[m], out_r.at[m], mirror)
+        return rdma(x_next.at[part(m)], state_ref.at[0, part(m)], out_s.at[m], out_r.at[m], back)
 
     def state_here(m):
         return pltpu.make_async_copy(x_next.at[part(m)], state_ref.at[0, part(m)], out_r.at[m])
@@ -318,7 +342,7 @@
             ).wait_recv()
             return total + y_in[k, m * rows:(m + 1) * rows].astype(F32)
 
-        first = x_all[t, m * rows:(m + 1) * rows].astype(F32)
+        first = x_all[own, m * rows:(m + 1) * rows].astype(F32)
         first = first + y_in[t, m * rows:(m + 1) * rows].astype(F32)
         x_next[m * rows:(m + 1) * rows] = lax.fori_loop(1, NT, add_y, first).astype(BF16)
 
@@ -326,16 +350,18 @@
         def _():
             core_send(m).start()
 
-        @pl.when(off_diag)
+        @pl.when(section == 1)
+        def _():
+            store_state(m)
+
+    def store_state(m):
+        @pl.when(moves)
         def _():
             state_send(m).start()
 
-        @pl.when(z == t)
+        @pl.when(z + t == 0)
         def _():
             state_here(m).start()
-
-    def cot_spread(i):
-        return rdma(c_all.at[t], c_all.at[t], cg_s.at[i], cg_r.at[t], to_tensor(tensor_at(i)))
 
     for m in range(PARTS):
         if m > 0:
@@ -346,39 +372,47 @@
         with jax.named_scope("up%d" % m):
             up_stage(m)
 
-    with jax.named_scope("waitcot"):
+    with jax.named_scope("after_up"):
         @pl.when(section == 0)
         def _():
             down_send.start()
-            go_on()
-
-        cot_in.wait_recv()
-
-        @pl.loop(1, NT)
-        def _(i):
-            cot_spread(i).start()
+
+        go_on()
 
     for m in range(PARTS):
         with jax.named_scope("hid%d" % m):
             hid_stage(m)
 
+    with jax.named_scope("waitcot"):
+        @pl.when(section == 0)
+        def _():
+            spread_cot()
+
     with jax.named_scope("waitdown"):
         down_here.wait()
         down_send.wait_recv()
 
-    for m in range(PARTS - 1):
-        with jax.named_scope("down%d" % m):
-            down_stage(m)
-        with jax.named_scope("next%d" % m):
-            next_stage(m)
-    with jax.named_scope("down%d" % (PARTS - 1)):
-        down_stage(PARTS - 1)
+    with jax.named_scope("down0"):
+        down_stage(0, 0, NZ)
+    with jax.named_scope("down1a"):
+        down_stage(1, 0, NZ // 2 + 1)
+    with jax.named_scope("next0"):
+        next_stage(0)
+    with jax.named_scope("down1b"):
+        down_stage(1, NZ // 2 + 1, NZ)
 
     with jax.named_scope("waitcg"):
         @pl.loop(1, NT)
         def _(i):
-            k = tensor_at(i)
-            rdma(c_all.at[k], c_all.at[k], cg_s.at[i], cg_r.at[k], to_tensor(k)).wait_recv()
+            k = block_at(i)
+
+            @pl.when(k != z)
+            def _():
+                rdma(
+                    c_all.at[k], c_all.at[k], cg_s.at[i], cg_r.at[k], to_tensor(tensor_at(i))
+                ).wait_recv()
+
+        cot_here.wait()
 
     def grad_half(which):
         hid_t = hid_all[...].reshape(NZ * tokens, hidden)
@@ -388,15 +422,12 @@
 
     grad_send = rdma(grad_out, grad_in, gr_s, gr_r, pair)
 
-    def grad_stage():
-        grad_out[...] = grad_half(1 - xl).astype(BF16)
-        grad_send.start()
-        grad_own[...] = grad_half(xl)
-
     with jax.named_scope("grad1"):
         @pl.when(section == 1)
         def _():
-            grad_stage()
+            grad_out[...] = grad_half(1 - xl).astype(BF16)
+            grad_send.start()
+            grad_own[...] = grad_half(xl)
 
     with jax.named_scope("next%d" % (PARTS - 1)):
         next_stage(PARTS - 1)
@@ -404,7 +435,12 @@
     with jax.named_scope("grad0"):
         @pl.when(section == 0)
         def _():
-            grad_stage()
+            grad_out[...] = grad_half(1 - xl).astype(BF16)
+            grad_own[...] = grad_half(xl)
+            pl.semaphore_wait(go, 1)
+            grad_send.start()
+            for m in range(PARTS):
+                store_state(m)
 
     with jax.named_scope("waitgrad"):
         grad_send.wait_recv()
@@ -418,15 +454,22 @@
             for m in range(PARTS):
                 core_send(m).wait_send()
 
-        @pl.when(off_diag & (section == 0))
+        @pl.when(moves & (section == 0))
         def _():
             for m in range(PARTS):
                 tok_send(m).wait_send()
 
-        @pl.when(off_diag)
+        @pl.when(shares_cot)
+        def _():
+            cot_send.wait_send()
+
+            @pl.loop(1, NT)
+            def _(i):
+                cot_spread(i).wait_send()
+
+        @pl.when(moves)
         def _():
             gain_send.wait_send()
-            cot_send.wait_send()
             for m in range(PARTS):
                 state_send(m).wait_send()
 
@@ -436,10 +479,9 @@
 
         @pl.loop(1, NT)
         def _(i):
-            cot_spread(i).wait_send()
             for m in range(PARTS):
                 spread(m, i).wait_send()
-                y_copy(m, tensor_at(i)).wait_send()
+                y_copy(m, block_at(i)).wait_send()
 
         @pl.loop(1, NZ)
         def _(i):
@@ -494,7 +536,7 @@
             pltpu.VMEM((hidden, half), BF16),
             pltpu.VMEM((hidden, half), BF16),
         ]
-        + [one] * 13
+        + [one] * 14
         + [dma((8,))] * 2
         + [dma((PARTS,))] * 5
         + [dma((8 * PARTS,))] * 10

time: 125 us -> 116 us (0.928)
  the two profiles are of different devices: /device:TPU:7 before, /device:TPU:55 now
where the time goes in v3:
time: 116 us
  Pallas kernels  112 us (97%)
  local copies, waits for them, and re-layouts  3.29 us (3%)
    pallas_call x1, Pallas kernels, body(): pl.pallas_call(run, out_shape=(jax.ShapeDtypeStruct((1, rows, feats), BF1...  112 us
    unnamed x2, local copies, waits for them, and re-layouts  3.29 us

profile of v3, /device:TPU:55, one launch (start us, length us, event | category | flops | bytes accessed | tf_op | source)
XLA Modules:
  0.0 115.7 jit_solution(5172629078626347717)
XLA Ops:
  0.6 111.8 %shard_map.68 = (bf16[1,128,512]{2,1,0:T(8,128)(2,1)}, bf16[1,640,256]{2,1,0:T(8,128)(2,1)}) custom-call(bf16[128,512]{1,0:T(8,128)(2,1)} %refs_0_.1, bf16[1,512]{1,0:T(2,128)(2,1)} %refs_1_.1, bf16[1,256,640]{2,1,0:T(8,128)(2,1)} %refs_2_.1, bf16[1,640,256]{2,1,0:T(8,128)(2,1)} %refs_3_.1, bf16[1,128,4096]{2,1,0:T(8,128)(2,1)} %refs_4_.1), custom_call_target="tpu_custom_call" | custom-call | tf_op jit(solution)/shard_map/pallas_call | solution.py:511
  112.4 1.6 %copy.9 = bf16[1,128,512]{2,1,0:T(8,128)(2,1)} copy(bf16[1,128,512]{2,1,0:T(8,128)(2,1)} %get-tuple-element.4) | data formatting | bytes 262144
  114.0 1.7 %copy.10 = bf16[1,640,256]{2,1,0:T(8,128)(2,1)} copy(bf16[1,640,256]{2,1,0:T(8,128)(2,1)} %get-tuple-element.5) | data formatting | bytes 655360

commit v4 on v3

--- a/solution.py
+++ b/solution.py
@@ -11,6 +11,7 @@
 NZ, NY, NX = 8, 4, 2
 NT = NY * NX
 PARTS = 2
+UP_SPLIT = 5
 F32, BF16 = jnp.float32, jnp.bfloat16
 
 
@@ -23,12 +24,14 @@
     tok_ref, gain_ref, up_ref, down_ref, cot_ref,
     state_ref, grad_ref,
     x_all, c_all, gain_z, up_pair, down_pair,
-    part_out, part_in, sq_out, sq_in, acc, hid_all, y_out, y_in, x_next,
+    part_out, part_own, part_in, sum_in, sum_out, relay, sq_out, sq_in, acc, hid_all,
+    y_out, y_in, x_next,
     grad_own, grad_out, grad_in, grad_done,
     gain_s, gain_r, cotp_s, cotp_r, up_s, up_r, down_s, down_r, upl, downl,
     gr_s, gr_r, gd_s, cotl, cg_s, cg_r,
     xin_s, xin_r, core_s, out_s, out_r,
-    ag_s, ag_r, rz_s, rz_r, sq_s, sq_r, az_s, az_r, rt_s, rt_r,
+    ag_s, ag_r, sq_s, sq_r, rt_s, rt_r,
+    rz_s, rz_r, sum_r, sum_s, az_s, az_r, rel_r, rel_s,
     go,
 ):
     section = lax.axis_index("section")
@@ -41,6 +44,7 @@
     feats = tok_ref.shape[1]
     tokens = tok_ref.shape[0]
     rows = tokens // PARTS
+    piece = rows // 2
     hidden = up_ref.shape[2]
     pair = {"xl": 1 - xl}
     core = {"section": 1 - section}
@@ -65,6 +69,9 @@
     def z_at(i):
         return (z + ring_offset(i) + NZ) % NZ
 
+    def helper(step):
+        return {"section": 1 - section, "z": (z + step + NZ) % NZ}
+
     def part(m):
         return pl.ds(m * rows, rows)
 
@@ -94,16 +101,20 @@
 
         pl.semaphore_signal(barrier, inc=1, device_id=pair, device_id_type=MESH)
         pl.semaphore_signal(barrier, inc=1, device_id=core, device_id_type=MESH)
+        for step in (1, -1, 2, -2):
+            pl.semaphore_signal(
+                barrier, inc=1, device_id=helper(step), device_id_type=MESH
+            )
 
         @pl.when(moves)
         def _():
             pl.semaphore_signal(barrier, inc=1, device_id=ahead, device_id_type=MESH)
             pl.semaphore_signal(barrier, inc=1, device_id=back, device_id_type=MESH)
-            pl.semaphore_wait(barrier, NZ + NT + 2)
+            pl.semaphore_wait(barrier, NZ + NT + 6)
 
         @pl.when(z + t == 0)
         def _():
-            pl.semaphore_wait(barrier, NZ + NT)
+            pl.semaphore_wait(barrier, NZ + NT + 4)
 
     def tok_send(m):
         return rdma(tok_ref.at[part(m)], x_all.at[z, part(m)], xin_s.at[m], xin_r.at[m], ahead)
@@ -131,19 +142,85 @@
         def _():
             cot_send.start()
 
+    beside = (y * NX + 1 - xh - z + NT) % NT
+
     def cot_spread(i):
         return rdma(
-            c_all.at[own], c_all.at[own], cg_s.at[i], cg_r.at[own], to_tensor(tensor_at(i))
+            c_all.at[own], c_all.at[own], cg_s.at[i - 1], cg_r.at[own], to_tensor(tensor_at(i))
+        )
+
+    def cot_pass(i):
+        return rdma(
+            c_all.at[beside], c_all.at[beside], cg_s.at[i + 3], cg_r.at[beside],
+            to_tensor(tensor_at(i)),
         )
 
     def spread_cot():
         @pl.when(shares_cot)
         def _():
             cot_in.wait_recv()
-
-            @pl.loop(1, NT)
-            def _(i):
+            for i in (NY, 1, 2, 3):
                 cot_spread(i).start()
+
+    def pass_cot():
+        @pl.when(beside != z)
+        def _():
+            ref = c_all.at[beside]
+            rdma(ref, ref, cg_s.at[0], cg_r.at[beside], pair).wait_recv()
+            for i in range(1, NY):
+                cot_pass(i).start()
+
+    def sum_wait(m, way, slot):
+        span = pl.ds(way * piece, piece) if slot == 2 else pl.ds(0, rows)
+        ref = sum_in.at[m, way, slot, span]
+        rdma(ref, ref, sum_s.at[0], sum_r.at[m * 6 + way * 3 + slot], core).wait_recv()
+
+    def sum_send(m, way):
+        return rdma(
+            sum_out.at[m, way], part_in.at[2 + way, part(m)],
+            sum_s.at[m * 2 + way], rz_r.at[m * 4 + 2 + way], helper(2 - 4 * way),
+        )
+
+    def relay_sum(m):
+        for way in range(2):
+            for slot in range(3):
+                sum_wait(m, way, slot)
+            for quarter in range(2):
+                span = slice(quarter * piece, (quarter + 1) * piece)
+                total = sum_in[m, way, 0, span].astype(F32) + sum_in[m, way, 1, span].astype(F32)
+                if quarter == way:
+                    total = total + sum_in[m, way, 2, span].astype(F32)
+                sum_out[m, way, span] = total.astype(BF16)
+            sum_send(m, way).start()
+
+    def relay_sends(m, way):
+        sign = 1 - 2 * way
+        block = (z - 2 * sign + NZ) % NZ
+        slot = m * 6 + way * 3
+        first = m * 8 + way * 4
+        span = pl.ds(way * piece, piece)
+        far = pl.ds(m * rows + way * piece, piece)
+        return (
+            rdma(
+                relay.at[m, way, span], hid_all.at[block, far],
+                rel_s.at[slot], az_r.at[first + 3], helper(2 * sign),
+            ),
+            rdma(
+                relay.at[m, way], hid_all.at[block, part(m)],
+                rel_s.at[slot + 1], az_r.at[first + 2], helper(sign),
+            ),
+            rdma(
+                relay.at[m, way], hid_all.at[block, part(m)],
+                rel_s.at[slot + 2], az_r.at[first + 1], core,
+            ),
+        )
+
+    def relay_hid(m):
+        for way in range(2):
+            ref = relay.at[m, way]
+            rdma(ref, ref, rel_s.at[0], rel_r.at[m * 2 + way], core).wait_recv()
+            for copy in relay_sends(m, way):
+                copy.start()
 
     def go_on():
         pl.semaphore_signal(go, inc=1, device_id=core, device_id_type=MESH)
@@ -178,10 +255,15 @@
         def _():
             pl.semaphore_wait(go, 1)
             start_cot()
+            relay_sum(0)
+            spread_cot()
             pl.semaphore_wait(go, 1)
+            relay_sum(1)
             up_send.start()
+            pass_cot()
+            relay_hid(0)
+            relay_hid(1)
             down_send.start()
-            spread_cot()
 
     def spread(m, i):
         return rdma(
@@ -211,10 +293,30 @@
         up_here.wait()
         up_send.wait_recv()
 
-    def part_copy(m, k):
-        return rdma(
-            part_out.at[k, part(m)], part_in.at[z, part(m)],
-            rz_s.at[m * NZ + k], rz_r.at[m * NZ + z], {"z": k},
+    def part_copies(m, k, way, dist):
+        sign = 1 - 2 * way
+        src = part_out.at[k, part(m)]
+        slot = m * 8 + way
+        if dist == 1:
+            return (rdma(src, part_in.at[way, part(m)], rz_s.at[slot], rz_r.at[m * 4 + way], {"z": k}),)
+        if dist == 2:
+            return (
+                rdma(src, sum_in.at[m, way, 0], rz_s.at[slot + 2], sum_r.at[m * 6 + way * 3], core),
+            )
+        if dist == 3:
+            return (
+                rdma(
+                    src, sum_in.at[m, way, 1], rz_s.at[slot + 4],
+                    sum_r.at[m * 6 + way * 3 + 1], helper(sign),
+                ),
+            )
+        return tuple(
+            rdma(
+                part_out.at[k, pl.ds(m * rows + w * piece, piece)],
+                sum_in.at[m, w, 2, pl.ds(w * piece, piece)],
+                rz_s.at[m * 8 + 6 + w], sum_r.at[m * 6 + w * 3 + 2], helper(2 - 4 * w),
+            )
+            for w in range(2)
         )
 
     def sq_copy(m, k):
@@ -222,10 +324,10 @@
             sq_out.at[m, k], sq_in.at[m, z], sq_s.at[m * NZ + k], sq_r.at[m * NZ + z], {"z": k}
         )
 
-    def up_stage(m):
+    def up_stage(m, first, last):
         gain_f = gain_z[...].astype(F32)
 
-        @pl.loop(0, NT)
+        @pl.loop(first, last)
         def _(i):
             k = block_at(i)
 
@@ -237,48 +339,69 @@
                 ).wait_recv()
 
             x_f = x_all[k, m * rows:(m + 1) * rows].astype(F32)
-            sq = jnp.concatenate([x_f * x_f] * PARTS, axis=0)
+            sq = x_f * x_f
+            sq = sum(sq[:, c:c + tokens] for c in range(0, feats, tokens))
+            sq = jnp.concatenate([sq] * PARTS, axis=0)
             sq_hi = sq.astype(BF16)
             sq_lo = (sq - sq_hi.astype(F32)).astype(BF16)
-            ones = jnp.ones((8, feats), BF16)
+            ones = jnp.ones((8, tokens), BF16)
             row_dims = (((1,), (1,)), ((), ()))
             sq_row = lax.dot_general(ones, sq_hi, row_dims, preferred_element_type=F32)
             sq_row = sq_row + lax.dot_general(ones, sq_lo, row_dims, preferred_element_type=F32)
             scaled = (x_f * gain_f).astype(BF16)
             value = jnp.dot(scaled, up_pair[...], preferred_element_type=F32).astype(BF16)
 
+            delta = (k - z + NZ) % NZ
+            way = delta // 5
+            dist = delta + way * (NZ - 2 * delta)
+
             @pl.when(k == z)
             def _():
-                part_in[k, m * rows:(m + 1) * rows] = value
+                part_own[m * rows:(m + 1) * rows] = value
                 sq_in[m, k] = sq_row
 
             @pl.when(k != z)
             def _():
                 part_out[k, m * rows:(m + 1) * rows] = value
                 sq_out[m, k] = sq_row
-                part_copy(m, k).start()
+
+            for far in range(1, 5):
+                @pl.when(dist == far)
+                def _():
+                    for copy in part_copies(m, k, way, far):
+                        copy.start()
+
+            @pl.when(k != z)
+            def _():
                 sq_copy(m, k).start()
 
-    def hid_spread(m, i):
-        return rdma(
-            hid_all.at[z, part(m)], hid_all.at[z, part(m)],
-            az_s.at[m * NZ + i], az_r.at[m * NZ + z], {"z": z_at(i)},
-        )
+    def hid_sends(m):
+        block = hid_all.at[z, part(m)]
+        out = []
+        for way in range(2):
+            sign = 1 - 2 * way
+            out.append(
+                rdma(block, relay.at[m, way], az_s.at[m * 4 + 2 + way], rel_r.at[m * 2 + way], helper(2 * sign))
+            )
+            out.append(
+                rdma(block, block, az_s.at[m * 4 + way], az_r.at[m * 8 + way * 4], {"z": (z + sign + NZ) % NZ})
+            )
+        return out
 
     def hid_stage(m):
-        acc[...] = part_in[z, m * rows:(m + 1) * rows].astype(F32)
+        span = slice(m * rows, (m + 1) * rows)
+        acc[...] = part_own[span].astype(F32)
+        for slot in range(4):
+            ref = part_in.at[slot, part(m)]
+            rdma(ref, ref, rz_s.at[0], rz_r.at[m * 4 + slot], core).wait_recv()
+            acc[...] += part_in[slot, span].astype(F32)
 
         def add_square(i, total):
             k = z_at(i)
-            rdma(
-                part_out.at[k, part(m)], part_in.at[k, part(m)],
-                rz_s.at[m * NZ + k], rz_r.at[m * NZ + k], {"z": k},
-            ).wait_recv()
             rdma(
                 sq_out.at[m, k], sq_in.at[m, k],
                 sq_s.at[m * NZ + k], sq_r.at[m * NZ + k], {"z": k},
             ).wait_recv()
-            acc[...] += part_in[k, m * rows:(m + 1) * rows].astype(F32)
             return total + sq_in[m, k]
 
         sq_sum = lax.fori_loop(1, NZ, add_square, sq_in[m, z])
@@ -287,9 +410,8 @@
         pre_act = acc[...] * lax.rsqrt(mean_col + EPS)
         hid_all[z, m * rows:(m + 1) * rows] = jax.nn.gelu(pre_act, approximate=True).astype(BF16)
 
-        @pl.loop(1, NZ)
-        def _(i):
-            hid_spread(m, i).start()
+        for copy in hid_sends(m):
+            copy.start()
 
     def y_copy(m, k):
         return rdma(
@@ -302,12 +424,17 @@
         def _(i):
             k = z_at(i)
 
-            @pl.when(i > 0)
-            def _():
-                rdma(
-                    hid_all.at[k, part(m)], hid_all.at[k, part(m)],
-                    az_s.at[m * NZ + i], az_r.at[m * NZ + k], {"z": k},
-                ).wait_recv()
+            @pl.when((i > 0) & (i < NZ - 1))
+            def _():
+                ref = hid_all.at[k, part(m)]
+                slot = m * 8 + (i % 2) * 4 + (i + 1) // 2 - 1
+                rdma(ref, ref, az_s.at[0], az_r.at[slot], core).wait_recv()
+
+            @pl.when(i == NZ - 1)
+            def _():
+                for way in range(2):
+                    ref = hid_all.at[k, pl.ds(m * rows + way * piece, piece)]
+                    rdma(ref, ref, az_s.at[0], az_r.at[m * 8 + way * 4 + 3], core).wait_recv()
 
             hid = hid_all[k, m * rows:(m + 1) * rows]
             y_lo = jnp.dot(hid, down_pair[0], preferred_element_type=F32).astype(BF16)
@@ -363,14 +490,16 @@
         def _():
             state_here(m).start()
 
-    for m in range(PARTS):
-        if m > 0:
-            with jax.named_scope("waitx%d" % m):
-                @pl.when(section == 1)
-                def _():
-                    take_x(m)
-        with jax.named_scope("up%d" % m):
-            up_stage(m)
+    with jax.named_scope("up0"):
+        up_stage(0, 0, UP_SPLIT)
+    with jax.named_scope("waitx1"):
+        @pl.when(section == 1)
+        def _():
+            take_x(1)
+    with jax.named_scope("up0b"):
+        up_stage(0, UP_SPLIT, NT)
+    with jax.named_scope("up1"):
+        up_stage(1, 0, NT)
 
     with jax.named_scope("after_up"):
         @pl.when(section == 0)
@@ -382,11 +511,6 @@
     for m in range(PARTS):
         with jax.named_scope("hid%d" % m):
             hid_stage(m)
-
-    with jax.named_scope("waitcot"):
-        @pl.when(section == 0)
-        def _():
-            spread_cot()
 
     with jax.named_scope("waitdown"):
         down_here.wait()
@@ -401,16 +525,15 @@
     with jax.named_scope("down1b"):
         down_stage(1, NZ // 2 + 1, NZ)
 
-    with jax.named_scope("waitcg"):
+    def wait_cot():
         @pl.loop(1, NT)
         def _(i):
             k = block_at(i)
 
-            @pl.when(k != z)
-            def _():
-                rdma(
-                    c_all.at[k], c_all.at[k], cg_s.at[i], cg_r.at[k], to_tensor(tensor_at(i))
-                ).wait_recv()
+            @pl.when((k != z) & (i != NY))
+            def _():
+                ref = c_all.at[k]
+                rdma(ref, ref, cg_s.at[0], cg_r.at[k], pair).wait_recv()
 
         cot_here.wait()
 
@@ -425,6 +548,7 @@
     with jax.named_scope("grad1"):
         @pl.when(section == 1)
         def _():
+            wait_cot()
             grad_out[...] = grad_half(1 - xl).astype(BF16)
             grad_send.start()
             grad_own[...] = grad_half(xl)
@@ -435,12 +559,19 @@
     with jax.named_scope("grad0"):
         @pl.when(section == 0)
         def _():
+            for m in range(PARTS):
+                relay_sum(m)
+            pl.semaphore_wait(go, 1)
+            spread_cot()
+            for m in range(PARTS):
+                store_state(m)
+            relay_hid(0)
+            pass_cot()
+            relay_hid(1)
+            wait_cot()
             grad_out[...] = grad_half(1 - xl).astype(BF16)
+            grad_send.start()
             grad_own[...] = grad_half(xl)
-            pl.semaphore_wait(go, 1)
-            grad_send.start()
-            for m in range(PARTS):
-                store_state(m)
 
     with jax.named_scope("waitgrad"):
         grad_send.wait_recv()
@@ -462,10 +593,13 @@
         @pl.when(shares_cot)
         def _():
             cot_send.wait_send()
-
-            @pl.loop(1, NT)
-            def _(i):
+            for i in range(1, NY + 1):
                 cot_spread(i).wait_send()
+
+        @pl.when(beside != z)
+        def _():
+            for i in range(1, NY):
+                cot_pass(i).wait_send()
 
         @pl.when(moves)
         def _():
@@ -486,9 +620,21 @@
         @pl.loop(1, NZ)
         def _(i):
             for m in range(PARTS):
-                part_copy(m, z_at(i)).wait_send()
                 sq_copy(m, z_at(i)).wait_send()
-                hid_spread(m, i).wait_send()
+
+        for m in range(PARTS):
+            for way in range(2):
+                for dist in range(1, 4):
+                    k = (z + dist * (1 - 2 * way) + NZ) % NZ
+                    for copy in part_copies(m, k, way, dist):
+                        copy.wait_send()
+                sum_send(m, way).wait_send()
+                for copy in relay_sends(m, way):
+                    copy.wait_send()
+            for copy in part_copies(m, (z + 4) % NZ, 0, 4):
+                copy.wait_send()
+            for copy in hid_sends(m):
+                copy.wait_send()
 
     with jax.named_scope("waitstate"):
         for m in range(PARTS):
@@ -523,7 +669,11 @@
             pltpu.VMEM((2 * half, hidden), BF16),
             pltpu.VMEM((2, hidden, half), BF16),
             pltpu.VMEM((NZ, rows, hidden), BF16),
-            pltpu.VMEM((NZ, rows, hidden), BF16),
+            pltpu.VMEM((rows, hidden), BF16),
+            pltpu.VMEM((4, rows, hidden), BF16),
+            pltpu.VMEM((PARTS, 2, 3, rows // PARTS, hidden), BF16),
+            pltpu.VMEM((PARTS, 2, rows // PARTS, hidden), BF16),
+            pltpu.VMEM((PARTS, 2, rows // PARTS, hidden), BF16),
             pltpu.VMEM((PARTS, NZ, 8, rows), F32),
             pltpu.VMEM((PARTS, NZ, 8, rows), F32),
             pltpu.VMEM((rows // PARTS, hidden), F32),
@@ -539,7 +689,8 @@
         + [one] * 14
         + [dma((8,))] * 2
         + [dma((PARTS,))] * 5
-        + [dma((8 * PARTS,))] * 10
+        + [dma((8 * PARTS,))] * 6
+        + [dma((n * PARTS,)) for n in (8, 4, 6, 2, 4, 8, 2, 6)]
         + [pltpu.SemaphoreType.REGULAR],
         compiler_params=pltpu.CompilerParams(
             collective_id=0, has_side_effects=True, vmem_limit_bytes=60 * 1024 * 1024

time: 116 us -> 106 us (0.914)
  the two profiles are of different devices: /device:TPU:55 before, /device:TPU:1 now
where the time goes in v4:
time: 106 us
  Pallas kernels  102 us (96%)
  local copies, waits for them, and re-layouts  3.29 us (3%)
    pallas_call x1, Pallas kernels, body(): pl.pallas_call(run, out_shape=(jax.ShapeDtypeStruct((1, rows, feats), BF1...  102 us
    unnamed x2, local copies, waits for them, and re-layouts  3.29 us

profile of v4, /device:TPU:1, one launch (start us, length us, event | category | flops | bytes accessed | tf_op | source)
XLA Modules:
  0.0 105.7 jit_solution(12849983531759543000)
XLA Ops:
  0.6 101.8 %shard_map.68 = (bf16[1,128,512]{2,1,0:T(8,128)(2,1)}, bf16[1,640,256]{2,1,0:T(8,128)(2,1)}) custom-call(bf16[128,512]{1,0:T(8,128)(2,1)} %refs_0_.1, bf16[1,512]{1,0:T(2,128)(2,1)} %refs_1_.1, bf16[1,256,640]{2,1,0:T(8,128)(2,1)} %refs_2_.1, bf16[1,640,256]{2,1,0:T(8,128)(2,1)} %refs_3_.1, bf16[1,128,4096]{2,1,0:T(8,128)(2,1)} %refs_4_.1), custom_call_target="tpu_custom_call" | custom-call | tf_op jit(solution)/shard_map/pallas_call | solution.py:657
  102.4 1.6 %copy.9 = bf16[1,128,512]{2,1,0:T(8,128)(2,1)} copy(bf16[1,128,512]{2,1,0:T(8,128)(2,1)} %get-tuple-element.4) | data formatting | bytes 262144
  104.0 1.7 %copy.10 = bf16[1,640,256]{2,1,0:T(8,128)(2,1)} copy(bf16[1,640,256]{2,1,0:T(8,128)(2,1)} %get-tuple-element.5) | data formatting | bytes 655360

commit v5 on v4

v5 whole, which is shorter than its diff:
```python
import jax
import jax.numpy as jnp
from jax import lax
from jax.experimental import pallas as pl
from jax.experimental.pallas import tpu as pltpu
from jax.sharding import Mesh
from jax.sharding import PartitionSpec as P

EPS = 1e-06
MESH = pl.DeviceIdType.MESH
NZ, NY, NX = 8, 4, 2
NT = NY * NX
F32, BF16 = jnp.float32, jnp.bfloat16

SIZES = (32,)*4
STARTS = tuple(sum(SIZES[:m]) for m in range(len(SIZES)))
PARTS = len(SIZES)


def order_of(section):
    gap = 4 / PARTS
    todo = []
    for m in range(PARTS):
        up0 = 18 + 2.5 * gap * m
        pass0 = 31 + 2.7 * gap * m
        down0 = 38 + 3 * gap * m
        up1 = 50 + 3 * gap * m
        if section == 0:
            todo += [(up0, "up", m), (up0 + 10, "hid", m), (down0, "down", m)]
            todo += [(down0 + 6.1, "next", m), (up1 + 4, "sum", m), (up1 + 11.5, "pass", m)]
        else:
            todo += [(up0 + 4, "sum", m), (pass0, "pass", m), (up1 - 5.9, "take", m)]
            todo += [(up1, "up", m), (up1 + 8.5, "hid", m), (up1 + 15.5, "down", m)]
            todo += [(up1 + 19.5, "next", m)]
    last = 50 + 3 * gap * (PARTS - 1)
    if section == 0:
        todo += [(18.1, "down_copy", 0), (18.2, "cot_spread", 0), (26, "cot_pass", 0)]
        todo += [(last + 1, "state", 0), (53.9, "grad", 0)]
    else:
        todo += [(25, "cot_spread", 0), (30.7, "up_copy", 0), (30.8, "cot_pass", 0)]
        todo += [(last + 0.1, "down_copy", 0), (last + 16, "grad", 0)]
    return [(name, m) for _, name, m in sorted(todo)]


def ring_offset(i):
    return ((i + 1) // 2) * (1 - 2 * ((i + 1) % 2))


def kernel(
    width,
    tok_ref, gain_ref, up_ref, down_ref, cot_ref,
    state_ref, grad_ref,
    x_all, c_all, gain_z, up_pair, down_pair,
    part_out, part_own, part_in, sum_in, sum_out, relay, sq_out, sq_in, hid_all,
    y_out, y_in, x_next, grad_own, grad_out, grad_in, grad_done,
    gain_s, gain_r, cotp_s, cotp_r, up_s, up_r, down_s, down_r, upl, downl,
    gr_s, gr_r, gd_s, cotl, cg_s, cg_r,
    xin_s, xin_r, core_s, out_s, out_r, sqh_s, sqh_r,
    ag_s, ag_r, sq_s, sq_r, rt_s, rt_r,
    rz_s, rz_r, sum_r, sum_s, az_s, az_r, rel_r, rel_s,
    go,
):
    section = lax.axis_index("section")
    z = lax.axis_index("z")
    xl = lax.axis_index("xl")
    y = lax.axis_index("y")
    xh = lax.axis_index("xh")
    t = y * NX + xh
    half = up_ref.shape[1]
    feats = tok_ref.shape[1]
    tokens = tok_ref.shape[0]
    hidden = up_ref.shape[2]
    pair = {"xl": 1 - xl}
    core = {"section": 1 - section}
    own = (t - z + NT) % NT
    ahead_t = (z + t) % NT
    ahead = {"z": t, "y": ahead_t // NX, "xh": ahead_t % NX}
    back = {"z": own, "y": z // NX, "xh": z % NX}
    moves = (z + t) > 0
    shares_cot = own != z

    def to_tensor(k):
        return {"y": k // NX, "xh": k % NX}

    def tensor_at(i):
        k = i % NY
        step = k + (k // 2) * (1 - 2 * (k % 2))
        return ((y + step) % NY) * NX + (xh + i // NY) % NX

    def block_at(i):
        return (tensor_at(i) - z + NT) % NT

    def z_at(i):
        return (z + ring_offset(i) + NZ) % NZ

    def helper(step):
        return {"section": 1 - section, "z": (z + step + NZ) % NZ}

    def part(m):
        return pl.ds(STARTS[m], SIZES[m])

    def span_of(m):
        return slice(STARTS[m], STARTS[m] + SIZES[m])

    def side(m, way):
        piece = SIZES[m] // 2
        return pl.ds(STARTS[m] + way * piece, piece)

    def rdma(src, dst, ssem, rsem, dev):
        return pltpu.make_async_remote_copy(
            src_ref=src, dst_ref=dst, send_sem=ssem, recv_sem=rsem,
            device_id=dev, device_id_type=MESH,
        )

    def arrived(ref, sem):
        rdma(ref, ref, gain_s, sem, core).wait_recv()

    def greet(dev):
        pl.semaphore_signal(barrier, inc=1, device_id=dev, device_id_type=MESH)

    with jax.named_scope("barrier"):
        mine = pl.ds(pl.multiple_of(xl * half, 128), half)
        up_here = pltpu.make_async_copy(up_ref.at[0], up_pair.at[mine], upl)
        down_here = pltpu.make_async_copy(down_ref.at[0], down_pair.at[xl], downl)
        up_here.start()
        down_here.start()
        barrier = pltpu.get_barrier_semaphore()

        @pl.loop(1, NZ)
        def _(i):
            greet({"z": z_at(i)})

        @pl.loop(1, NT)
        def _(i):
            greet(to_tensor(tensor_at(i)))

        greet(pair)
        greet(core)
        for step in (1, -1, 2, -2):
            greet(helper(step))

        @pl.when(moves)
        def _():
            greet(ahead)
            greet(back)
            pl.semaphore_wait(barrier, NZ + NT + 6)

        @pl.when(z + t == 0)
        def _():
            pl.semaphore_wait(barrier, NZ + NT + 4)

    def tok_send(m):
        return rdma(tok_ref.at[part(m)], x_all.at[z, part(m)], xin_s.at[m], xin_r.at[m], ahead)

    def tok_here(m):
        return pltpu.make_async_copy(tok_ref.at[part(m)], x_all.at[own, part(m)], xin_r.at[m])

    gain_send = rdma(gain_ref, gain_z, gain_s, gain_r, ahead)
    gain_here = pltpu.make_async_copy(gain_ref, gain_z, gain_r)

    def cot_cols(k):
        return cot_ref.at[0, :, pl.ds(pl.multiple_of(k * feats, 128), feats)]

    cot_send = rdma(cot_cols(own), c_all.at[z], cotp_s, cotp_r, {"z": own})
    cot_here = pltpu.make_async_copy(cot_cols(z), c_all.at[z], cotl)
    up_send = rdma(up_ref.at[0], up_pair.at[mine], up_s, up_r, pair)
    down_send = rdma(down_ref.at[0], down_pair.at[xl], down_s, down_r, pair)
    grad_send = rdma(grad_out, grad_in, gr_s, gr_r, pair)

    def start_cot():
        @pl.when(shares_cot)
        def _():
            cot_send.start()

    beside = (y * NX + 1 - xh - z + NT) % NT

    def cot_spread(i):
        return rdma(
            c_all.at[own], c_all.at[own], cg_s.at[i - 1], cg_r.at[own], to_tensor(tensor_at(i))
        )

    def cot_pass(i):
        return rdma(
            c_all.at[beside], c_all.at[beside], cg_s.at[i + 3], cg_r.at[beside],
            to_tensor(tensor_at(i)),
        )

    def spread_cot():
        @pl.when(shares_cot)
        def _():
            arrived(c_all.at[own], cotp_r)
            for i in (NY, 1, 2, 3):
                cot_spread(i).start()

    def pass_cot():
        @pl.when(beside != z)
        def _():
            arrived(c_all.at[beside], cg_r.at[beside])
            for i in range(1, NY):
                cot_pass(i).start()

    def wait_cot():
        @pl.loop(1, NT)
        def _(i):
            k = block_at(i)

            @pl.when((k != z) & (i != NY))
            def _():
                arrived(c_all.at[k], cg_r.at[k])

        cot_here.wait()

    def sum_send(m, way):
        return rdma(
            sum_out.at[way, part(m)], part_in.at[2 + way, part(m)],
            sum_s.at[m * 2 + way], rz_r.at[m * 4 + 2 + way], helper(2 - 4 * way),
        )

    def sum_stage(m):
        for way in range(2):
            first = m * 6 + way * 3
            arrived(sum_in.at[way, 0, part(m)], sum_r.at[first])
            arrived(sum_in.at[way, 1, part(m)], sum_r.at[first + 1])
            arrived(sum_in.at[way, 2, side(m, way)], sum_r.at[first + 2])
            for which in range(2):
                piece = SIZES[m] // 2
                rows = slice(STARTS[m] + which * piece, STARTS[m] + (which + 1) * piece)
                total = sum_in[way, 0, rows].astype(F32) + sum_in[way, 1, rows].astype(F32)
                if which == way:
                    total = total + sum_in[way, 2, rows].astype(F32)
                sum_out[way, rows] = total.astype(BF16)
            sum_send(m, way).start()

    def relay_sends(m, way):
        sign = 1 - 2 * way
        block = (z - 2 * sign + NZ) % NZ
        slot = m * 6 + way * 3
        first = m * 8 + way * 4
        full = relay.at[way, part(m)]
        whole = hid_all.at[block, part(m)]
        return (
            rdma(
                relay.at[way, side(m, way)], hid_all.at[block, side(m, way)],
                rel_s.at[slot], az_r.at[first + 3], helper(2 * sign),
            ),
            rdma(full, whole, rel_s.at[slot + 1], az_r.at[first + 2], helper(sign)),
            rdma(full, whole, rel_s.at[slot + 2], az_r.at[first + 1], core),
        )

    def pass_stage(m):
        for way in range(2):
            arrived(relay.at[way, part(m)], rel_r.at[m * 2 + way])
            for copy in relay_sends(m, way):
                copy.start()

    def spread(m, i):
        return rdma(
            x_all.at[own, part(m)], x_all.at[own, part(m)],
            ag_s.at[m * NT + i], ag_r.at[m * NT + own], to_tensor(tensor_at(i)),
        )

    def sq_copy(m):
        return rdma(sq_out.at[m], sq_in.at[m, z], sqh_s.at[m], sqh_r.at[m], {"z": own})

    def sq_spread(m, i):
        return rdma(
            sq_in.at[m, own], sq_in.at[m, own],
            sq_s.at[m * NT + i], sq_r.at[m * NT + own], to_tensor(tensor_at(i)),
        )

    def sq_stage(m):
        @pl.when(shares_cot)
        def _():
            arrived(sq_in.at[m, own], sqh_r.at[m])

        @pl.loop(1, NT)
        def _(i):
            sq_spread(m, i).start()

    def take_stage(m):
        arrived(x_all.at[own, part(m)], xin_r.at[m])

        @pl.loop(1, NT)
        def _(i):
            spread(m, i).start()

        x_f = x_all[own, span_of(m)].astype(F32)
        sq = x_f * x_f
        sq = sum(sq[:, c:c + tokens] for c in range(0, feats, tokens))
        sq = jnp.concatenate([sq] * (tokens // SIZES[m]), axis=0)
        sq_hi = sq.astype(BF16)
        sq_lo = (sq - sq_hi.astype(F32)).astype(BF16)
        ones = jnp.ones((8, tokens), BF16)
        row_dims = (((1,), (1,)), ((), ()))
        sq_row = lax.dot_general(ones, sq_hi, row_dims, preferred_element_type=F32)
        sq_row = sq_row + lax.dot_general(ones, sq_lo, row_dims, preferred_element_type=F32)
        sq_out[m] = sq_row

        @pl.when(own == z)
        def _():
            sq_in[m, z] = sq_row

        @pl.when(shares_cot)
        def _():
            sq_copy(m).start()

    def part_copies(m, k, way, dist):
        sign = 1 - 2 * way
        src = part_out.at[k, part(m)]
        slot = m * 8 + way
        first = m * 6 + way * 3
        if dist == 1:
            dst = part_in.at[way, part(m)]
            return (rdma(src, dst, rz_s.at[slot], rz_r.at[m * 4 + way], {"z": k}),)
        if dist == 2:
            return (rdma(src, sum_in.at[way, 0, part(m)], rz_s.at[slot + 2], sum_r.at[first], core),)
        if dist == 3:
            dst = sum_in.at[way, 1, part(m)]
            return (rdma(src, dst, rz_s.at[slot + 4], sum_r.at[first + 1], helper(sign)),)
        return tuple(
            rdma(
                part_out.at[k, side(m, w)], sum_in.at[w, 2, side(m, w)],
                rz_s.at[m * 8 + 6 + w], sum_r.at[m * 6 + w * 3 + 2], helper(2 - 4 * w),
            )
            for w in range(2)
        )

    def up_stage(m):
        sq_stage(m)
        gain_f = gain_z[...].astype(F32)
        rows = SIZES[m]

        @pl.loop(0, NT // 2)
        def _(j):
            scaled = []
            for i in (2 * j, 2 * j + 1):
                k = block_at(i)

                @pl.when(i > 0)
                def _():
                    arrived(x_all.at[k, part(m)], ag_r.at[m * NT + k])

                scaled.append((x_all[k, span_of(m)].astype(F32) * gain_f).astype(BF16))
            both = jnp.dot(
                jnp.concatenate(scaled, axis=0), up_pair[...], preferred_element_type=F32
            ).astype(BF16)
            for n in range(2):
                k = block_at(2 * j + n)
                value = both[n * rows:(n + 1) * rows]
                delta = (k - z + NZ) % NZ
                way = delta // 5
                dist = delta + way * (NZ - 2 * delta)

                @pl.when(k == z)
                def _():
                    part_own[span_of(m)] = value

                @pl.when(k != z)
                def _():
                    part_out[k, span_of(m)] = value

                for far in range(1, 5):
                    @pl.when(dist == far)
                    def _():
                        for copy in part_copies(m, k, way, far):
                            copy.start()

    def hid_sends(m):
        block = hid_all.at[z, part(m)]
        out = []
        for way in range(2):
            sign = 1 - 2 * way
            out.append(
                rdma(
                    block, relay.at[way, part(m)], az_s.at[m * 4 + 2 + way],
                    rel_r.at[m * 2 + way], helper(2 * sign),
                )
            )
            out.append(
                rdma(
                    block, block, az_s.at[m * 4 + way], az_r.at[m * 8 + way * 4],
                    {"z": (z + sign + NZ) % NZ},
                )
            )
        return out

    def hid_stage(m):
        rows = SIZES[m]

        @pl.loop(1, NT)
        def _(i):
            k = block_at(i)
            arrived(sq_in.at[m, k], sq_r.at[m * NT + k])

        for slot in range(4):
            arrived(part_in.at[slot, part(m)], rz_r.at[m * 4 + slot])
        total = part_own[span_of(m)].astype(F32)
        for slot in range(4):
            total = total + part_in[slot, span_of(m)].astype(F32)
        sq_sum = sum(sq_in[m, k] for k in range(NZ))
        square = jnp.transpose(jnp.broadcast_to(sq_sum[0:1, :], (tokens, tokens)))
        mean_col = square[0:rows, 0:1] / width
        pre_act = total * lax.rsqrt(mean_col + EPS)
        hid_all[z, span_of(m)] = jax.nn.gelu(pre_act, approximate=True).astype(BF16)
        for copy in hid_sends(m):
            copy.start()

    def y_copy(m, k):
        return rdma(
            y_out.at[k, part(m)], y_in.at[t, part(m)],
            rt_s.at[m * NT + k], rt_r.at[m * NT + t], to_tensor((k + z) % NT),
        )

    def down_stage(m):
        rows = SIZES[m]

        @pl.loop(0, NZ // 2)
        def _(j):
            hid = []
            for i in (2 * j, 2 * j + 1):
                k = z_at(i)

                @pl.when((i > 0) & (i < NZ - 1))
                def _():
                    slot = m * 8 + (i % 2) * 4 + (i + 1) // 2 - 1
                    arrived(hid_all.at[k, part(m)], az_r.at[slot])

                @pl.when(i == NZ - 1)
                def _():
                    for way in range(2):
                        arrived(hid_all.at[k, side(m, way)], az_r.at[m * 8 + way * 4 + 3])

                hid.append(hid_all[k, span_of(m)])
            hid = jnp.concatenate(hid, axis=0)
            y_lo = jnp.dot(hid, down_pair[0], preferred_element_type=F32).astype(BF16)
            y_hi = jnp.dot(hid, down_pair[1], preferred_element_type=F32).astype(BF16)
            for n in range(2):
                k = z_at(2 * j + n)
                rng = slice(n * rows, (n + 1) * rows)

                @pl.when(k == own)
                def _():
                    y_in[t, span_of(m), 0:half] = y_lo[rng]
                    y_in[t, span_of(m), half:] = y_hi[rng]

                @pl.when(k != own)
                def _():
                    y_out[k, span_of(m), 0:half] = y_lo[rng]
                    y_out[k, span_of(m), half:] = y_hi[rng]
                    y_copy(m, k).start()

    def core_send(m):
        return rdma(x_next.at[part(m)], x_all.at[own, part(m)], core_s.at[m], xin_r.at[m], core)

    def state_send(m):
        return rdma(x_next.at[part(m)], state_ref.at[0, part(m)], out_s.at[m], out_r.at[m], back)

    def state_here(m):
        return pltpu.make_async_copy(x_next.at[part(m)], state_ref.at[0, part(m)], out_r.at[m])

    def store_state(m):
        @pl.when(moves)
        def _():
            state_send(m).start()

        @pl.when(z + t == 0)
        def _():
            state_here(m).start()

    def next_stage(m, first_section):
        @pl.loop(1, NT)
        def _(i):
            k = tensor_at(i)
            arrived(y_in.at[k, part(m)], rt_r.at[m * NT + k])

        total = x_all[own, span_of(m)].astype(F32)
        for k in range(NT):
            total = total + y_in[k, span_of(m)].astype(F32)
        x_next[span_of(m)] = total.astype(BF16)
        if first_section:
            core_send(m).start()
        else:
            store_state(m)

    def grad_half(which):
        hid_t = hid_all[...].reshape(NZ * tokens, hidden)
        cols = pl.ds(pl.multiple_of(which * half, 128), half)
        cot = c_all[:, :, cols].reshape(NZ * tokens, half)
        return lax.dot_general(hid_t, cot, (((0,), (0,)), ((), ())), preferred_element_type=F32)

    def grad_stage():
        wait_cot()
        grad_out[...] = grad_half(1 - xl).astype(BF16)
        grad_send.start()
        grad_own[...] = grad_half(xl)

    def wait_up():
        arrived(gain_z, gain_r)
        up_here.wait()
        up_send.wait_recv()

    def wait_down():
        down_here.wait()
        down_send.wait_recv()

    def run(which):
        met = set()
        for name, m in order_of(which):
            with jax.named_scope("%s%d" % (name, m)):
                if name == "up" and name not in met:
                    wait_up()
                if name == "down" and name not in met:
                    wait_down()
                met.add(name)
                if name == "take":
                    take_stage(m)
                elif name == "up":
                    up_stage(m)
                elif name == "sum":
                    sum_stage(m)
                elif name == "hid":
                    hid_stage(m)
                elif name == "pass":
                    pass_stage(m)
                elif name == "down":
                    down_stage(m)
                elif name == "next":
                    next_stage(m, which == 0)
                elif name == "up_copy":
                    up_send.start()
                elif name == "down_copy":
                    down_send.start()
                elif name == "cot_spread":
                    spread_cot()
                elif name == "cot_pass":
                    pass_cot()
                elif name == "state":
                    for n in range(PARTS):
                        store_state(n)
                elif name == "grad":
                    grad_stage()

    cot_here.start()

    @pl.when(moves)
    def _():
        gain_send.start()

    @pl.when(z + t == 0)
    def _():
        gain_here.start()

    @pl.when(section == 0)
    def _():
        with jax.named_scope("send0"):
            @pl.when(moves)
            def _():
                for m in range(PARTS):
                    tok_send(m).start()

            @pl.when(z + t == 0)
            def _():
                for m in range(PARTS):
                    tok_here(m).start()

            up_send.start()

        with jax.named_scope("waitx"):
            for m in range(PARTS):
                take_stage(m)
            start_cot()
            pl.semaphore_signal(go, inc=1, device_id=core, device_id_type=MESH)
        run(0)

    @pl.when(section == 1)
    def _():
        with jax.named_scope("waitgo"):
            pl.semaphore_wait(go, 1)
            start_cot()
        run(1)

    with jax.named_scope("waitgrad"):
        grad_send.wait_recv()
        grad_done[...] = (grad_own[...] + grad_in[...].astype(F32)).astype(BF16)
        grad_store = pltpu.make_async_copy(grad_done, grad_ref.at[0], gd_s)
        grad_store.start()

    with jax.named_scope("drain"):
        @pl.when(section == 0)
        def _():
            for m in range(PARTS):
                core_send(m).wait_send()

        @pl.when(moves & (section == 0))
        def _():
            for m in range(PARTS):
                tok_send(m).wait_send()

        @pl.when(shares_cot)
        def _():
            cot_send.wait_send()
            for i in range(1, NY + 1):
                cot_spread(i).wait_send()

        @pl.when(beside != z)
        def _():
            for i in range(1, NY):
                cot_pass(i).wait_send()

        @pl.when(moves)
        def _():
            gain_send.wait_send()
            for m in range(PARTS):
                state_send(m).wait_send()

        up_send.wait_send()
        down_send.wait_send()
        grad_send.wait_send()

        @pl.loop(1, NT)
        def _(i):
            for m in range(PARTS):
                spread(m, i).wait_send()
                sq_spread(m, i).wait_send()
                y_copy(m, block_at(i)).wait_send()

        @pl.when(shares_cot)
        def _():
            for m in range(PARTS):
                sq_copy(m).wait_send()

        for m in range(PARTS):
            for way in range(2):
                for dist in range(1, 4):
                    k = (z + dist * (1 - 2 * way) + NZ) % NZ
                    for copy in part_copies(m, k, way, dist):
                        copy.wait_send()
                sum_send(m, way).wait_send()
                for copy in relay_sends(m, way):
                    copy.wait_send()
            for copy in part_copies(m, (z + 4) % NZ, 0, 4):
                copy.wait_send()
            for copy in hid_sends(m):
                copy.wait_send()

    with jax.named_scope("waitstate"):
        for m in range(PARTS):
            arrived(state_ref.at[0, part(m)], out_r.at[m])
        grad_store.wait()


def body(tokens, gain, w_up, w_down, cotangent):
    rows, feats = tokens.shape
    half, hidden = w_up.shape[1:]
    width = cotangent.shape[2]
    dma = pltpu.SemaphoreType.DMA
    hbm = pl.BlockSpec(memory_space=pl.ANY)

    def run(*refs):
        kernel(width, *refs)

    one = dma(())
    states, grads = pl.pallas_call(
        run,
        out_shape=(
            jax.ShapeDtypeStruct((1, rows, feats), BF16),
            jax.ShapeDtypeStruct((1, hidden, half), BF16),
        ),
        in_specs=[hbm] * 5,
        out_specs=(hbm, hbm),
        scratch_shapes=[
            pltpu.VMEM((NT, rows, feats), BF16),
            pltpu.VMEM((NT, rows, feats), BF16),
            pltpu.VMEM((1, feats), BF16),
            pltpu.VMEM((2 * half, hidden), BF16),
            pltpu.VMEM((2, hidden, half), BF16),
            pltpu.VMEM((NZ, rows, hidden), BF16),
            pltpu.VMEM((rows, hidden), BF16),
            pltpu.VMEM((4, rows, hidden), BF16),
            pltpu.VMEM((2, 3, rows, hidden), BF16),
            pltpu.VMEM((2, rows, hidden), BF16),
            pltpu.VMEM((2, rows, hidden), BF16),
            pltpu.VMEM((PARTS, 8, rows), F32),
            pltpu.VMEM((PARTS, NZ, 8, rows), F32),
            pltpu.VMEM((NZ, rows, hidden), BF16),
            pltpu.VMEM((NT, rows, feats), BF16),
            pltpu.VMEM((NT, rows, feats), BF16),
            pltpu.VMEM((rows, feats), BF16),
            pltpu.VMEM((hidden, half), F32),
            pltpu.VMEM((hidden, half), BF16),
            pltpu.VMEM((hidden, half), BF16),
            pltpu.VMEM((hidden, half), BF16),
        ]
        + [one] * 14
        + [dma((8,))] * 2
        + [dma((PARTS,))] * 7
        + [dma((8 * PARTS,))] * 6
        + [dma((n * PARTS,)) for n in (8, 4, 6, 2, 4, 8, 2, 6)]
        + [pltpu.SemaphoreType.REGULAR],
        compiler_params=pltpu.CompilerParams(
            collective_id=0, has_side_effects=True, vmem_limit_bytes=60 * 1024 * 1024
        ),
    )(tokens, gain, w_up, w_down, cotangent)
    return states, grads


def solution(mesh):
    torus = Mesh(
        mesh.devices.reshape(mesh.shape["section"], NZ, 2, NY, NX),
        ("section", "z", "xl", "y", "xh"),
    )
    dp, tensor = ("z", "xl"), ("y", "xh")
    in_specs = (
        P(dp, tensor),
        P("section", tensor),
        P("section", dp, tensor),
        P("section", tensor, dp),
        P("section", dp, None),
    )
    out_specs = (P("section", dp, tensor), P("section", tensor, dp))
    return jax.shard_map(body, mesh=torus, in_specs=in_specs, out_specs=out_specs, check_vma=False)
```

time: 106 us -> 102 us (0.962); the launches traced: 106 us -> 100 us
  Pallas kernels: 102 us -> 96.5 us
    pallas_call x1, Pallas kernels: 102 us -> 96.5 us  [body(): pl.pallas_call(run, out_shape=(jax.ShapeDtypeStruct((1, rows, feats), BF1...]
where the time goes in v5:
time: 102 us; the launch traced here: 100 us
  Pallas kernels  96.5 us (95%)
  local copies, waits for them, and re-layouts  3.29 us (3%)
    pallas_call x1, Pallas kernels, body(): pl.pallas_call(run, out_shape=(jax.ShapeDtypeStruct((1, rows, feats), BF1...  96.5 us
    unnamed x2, local copies, waits for them, and re-layouts  3.29 us

profile of v5, /device:TPU:1, one launch (start us, length us, event | category | flops | bytes accessed | tf_op | source)
XLA Modules:
  0.0 100.5 jit_solution(16648845837098164386)
XLA Ops:
  0.6 96.5 %shard_map.68 = (bf16[1,128,512]{2,1,0:T(8,128)(2,1)}, bf16[1,640,256]{2,1,0:T(8,128)(2,1)}) custom-call(bf16[128,512]{1,0:T(8,128)(2,1)} %refs_0_.1, bf16[1,512]{1,0:T(2,128)(2,1)} %refs_1_.1, bf16[1,256,640]{2,1,0:T(8,128)(2,1)} %refs_2_.1, bf16[1,640,256]{2,1,0:T(8,128)(2,1)} %refs_3_.1, bf16[1,128,4096]{2,1,0:T(8,128)(2,1)} %refs_4_.1), custom_call_target="tpu_custom_call" | custom-call | tf_op jit(solution)/shard_map/pallas_call | solution.py:663
  97.2 1.6 %copy.9 = bf16[1,128,512]{2,1,0:T(8,128)(2,1)} copy(bf16[1,128,512]{2,1,0:T(8,128)(2,1)} %get-tuple-element.4) | data formatting | bytes 262144
  98.7 1.7 %copy.10 = bf16[1,640,256]{2,1,0:T(8,128)(2,1)} copy(bf16[1,640,256]{2,1,0:T(8,128)(2,1)} %get-tuple-element.5) | data formatting | bytes 655360

commit v6 on v5

--- a/solution.py
+++ b/solution.py
@@ -29,12 +29,12 @@
             todo += [(up0, "up", m), (up0 + 10, "hid", m), (down0, "down", m)]
             todo += [(down0 + 6.1, "next", m), (up1 + 4, "sum", m), (up1 + 11.5, "pass", m)]
         else:
-            todo += [(up0 + 4, "sum", m), (pass0, "pass", m), (up1 - 5.9, "take", m)]
+            todo += [(up0 + 4, "sum", m), (pass0, "pass", m), (up1 - 6.1, "take", m)]
             todo += [(up1, "up", m), (up1 + 8.5, "hid", m), (up1 + 15.5, "down", m)]
             todo += [(up1 + 19.5, "next", m)]
     last = 50 + 3 * gap * (PARTS - 1)
     if section == 0:
-        todo += [(18.1, "down_copy", 0), (18.2, "cot_spread", 0), (26, "cot_pass", 0)]
+        todo += [(18.1, "down_copy", 0), (18.2, "cot_spread", 0), (31, "cot_pass", 0)]
         todo += [(last + 1, "state", 0), (53.9, "grad", 0)]
     else:
         todo += [(25, "cot_spread", 0), (30.7, "up_copy", 0), (30.8, "cot_pass", 0)]
@@ -54,10 +54,9 @@
     part_out, part_own, part_in, sum_in, sum_out, relay, sq_out, sq_in, hid_all,
     y_out, y_in, x_next, grad_own, grad_out, grad_in, grad_done,
     gain_s, gain_r, cotp_s, cotp_r, up_s, up_r, down_s, down_r, upl, downl,
-    gr_s, gr_r, gd_s, cotl, cg_s, cg_r,
-    xin_s, xin_r, core_s, out_s, out_r, sqh_s, sqh_r,
-    ag_s, ag_r, sq_s, sq_r, rt_s, rt_r,
-    rz_s, rz_r, sum_r, sum_s, az_s, az_r, rel_r, rel_s,
+    gr_s, gr_r, gd_s, cotl, cg_s, cp_s, cg_r,
+    xin_s, core_s, out_s, out_r, sqh_s, ag_s, sq_s, rt_s, rz_s, sum_s, az_s, rel_s,
+    xin_r, sqh_r, ag_r, sq_r, rt_r, rz_r, sum_r, az_r, rel_r,
     go,
 ):
     section = lax.axis_index("section")
@@ -150,7 +149,7 @@
             pl.semaphore_wait(barrier, NZ + NT + 4)
 
     def tok_send(m):
-        return rdma(tok_ref.at[part(m)], x_all.at[z, part(m)], xin_s.at[m], xin_r.at[m], ahead)
+        return rdma(tok_ref.at[part(m)], x_all.at[z, part(m)], xin_s, xin_r.at[m], ahead)
 
     def tok_here(m):
         return pltpu.make_async_copy(tok_ref.at[part(m)], x_all.at[own, part(m)], xin_r.at[m])
@@ -176,12 +175,12 @@
 
     def cot_spread(i):
         return rdma(
-            c_all.at[own], c_all.at[own], cg_s.at[i - 1], cg_r.at[own], to_tensor(tensor_at(i))
+            c_all.at[own], c_all.at[own], cg_s, cg_r.at[own], to_tensor(tensor_at(i))
         )
 
     def cot_pass(i):
         return rdma(
-            c_all.at[beside], c_all.at[beside], cg_s.at[i + 3], cg_r.at[beside],
+            c_all.at[beside], c_all.at[beside], cp_s, cg_r.at[beside],
             to_tensor(tensor_at(i)),
         )
 
@@ -213,15 +212,12 @@
     def sum_send(m, way):
         return rdma(
             sum_out.at[way, part(m)], part_in.at[2 + way, part(m)],
-            sum_s.at[m * 2 + way], rz_r.at[m * 4 + 2 + way], helper(2 - 4 * way),
+            sum_s, rz_r.at[m], helper(2 - 4 * way),
         )
 
     def sum_stage(m):
         for way in range(2):
-            first = m * 6 + way * 3
-            arrived(sum_in.at[way, 0, part(m)], sum_r.at[first])
-            arrived(sum_in.at[way, 1, part(m)], sum_r.at[first + 1])
-            arrived(sum_in.at[way, 2, side(m, way)], sum_r.at[first + 2])
+            arrived(part_out.at[0, pl.ds(0, SIZES[m] * 5 // 2)], sum_r.at[m * 2 + way])
             for which in range(2):
                 piece = SIZES[m] // 2
                 rows = slice(STARTS[m] + which * piece, STARTS[m] + (which + 1) * piece)
@@ -234,17 +230,16 @@
     def relay_sends(m, way):
         sign = 1 - 2 * way
         block = (z - 2 * sign + NZ) % NZ
-        slot = m * 6 + way * 3
         first = m * 8 + way * 4
         full = relay.at[way, part(m)]
         whole = hid_all.at[block, part(m)]
         return (
             rdma(
                 relay.at[way, side(m, way)], hid_all.at[block, side(m, way)],
-                rel_s.at[slot], az_r.at[first + 3], helper(2 * sign),
+                rel_s, az_r.at[first + 3], helper(2 * sign),
             ),
-            rdma(full, whole, rel_s.at[slot + 1], az_r.at[first + 2], helper(sign)),
-            rdma(full, whole, rel_s.at[slot + 2], az_r.at[first + 1], core),
+            rdma(full, whole, rel_s, az_r.at[first + 2], helper(sign)),
+            rdma(full, whole, rel_s, az_r.at[first + 1], core),
         )
 
     def pass_stage(m):
@@ -256,16 +251,16 @@
     def spread(m, i):
         return rdma(
             x_all.at[own, part(m)], x_all.at[own, part(m)],
-            ag_s.at[m * NT + i], ag_r.at[m * NT + own], to_tensor(tensor_at(i)),
+            ag_s, ag_r.at[m * NT + own], to_tensor(tensor_at(i)),
         )
 
     def sq_copy(m):
-        return rdma(sq_out.at[m], sq_in.at[m, z], sqh_s.at[m], sqh_r.at[m], {"z": own})
+        return rdma(sq_out.at[m], sq_in.at[m, z], sqh_s, sqh_r.at[m], {"z": own})
 
     def sq_spread(m, i):
         return rdma(
             sq_in.at[m, own], sq_in.at[m, own],
-            sq_s.at[m * NT + i], sq_r.at[m * NT + own], to_tensor(tensor_at(i)),
+            sq_s, sq_r.at[m], to_tensor(tensor_at(i)),
         )
 
     def sq_stage(m):
@@ -307,33 +302,33 @@
     def part_copies(m, k, way, dist):
         sign = 1 - 2 * way
         src = part_out.at[k, part(m)]
-        slot = m * 8 + way
-        first = m * 6 + way * 3
+        summed = sum_r.at[m * 2 + way]
         if dist == 1:
             dst = part_in.at[way, part(m)]
-            return (rdma(src, dst, rz_s.at[slot], rz_r.at[m * 4 + way], {"z": k}),)
+            return (rdma(src, dst, rz_s, rz_r.at[m], {"z": k}),)
         if dist == 2:
-            return (rdma(src, sum_in.at[way, 0, part(m)], rz_s.at[slot + 2], sum_r.at[first], core),)
+            return (rdma(src, sum_in.at[way, 0, part(m)], rz_s, summed, core),)
         if dist == 3:
             dst = sum_in.at[way, 1, part(m)]
-            return (rdma(src, dst, rz_s.at[slot + 4], sum_r.at[first + 1], helper(sign)),)
+            return (rdma(src, dst, rz_s, summed, helper(sign)),)
         return tuple(
             rdma(
                 part_out.at[k, side(m, w)], sum_in.at[w, 2, side(m, w)],
-                rz_s.at[m * 8 + 6 + w], sum_r.at[m * 6 + w * 3 + 2], helper(2 - 4 * w),
+                rz_s, sum_r.at[m * 2 + w], helper(2 - 4 * w),
             )
             for w in range(2)
         )
 
     def up_stage(m):
-        sq_stage(m)
         gain_f = gain_z[...].astype(F32)
         rows = SIZES[m]
-
-        @pl.loop(0, NT // 2)
+        group = 4 if m else 2
+
+        @pl.loop(0, NT // group)
         def _(j):
             scaled = []
-            for i in (2 * j, 2 * j + 1):
+            for n in range(group):
+                i = group * j + n
                 k = block_at(i)
 
                 @pl.when(i > 0)
@@ -344,8 +339,8 @@
             both = jnp.dot(
                 jnp.concatenate(scaled, axis=0), up_pair[...], preferred_element_type=F32
             ).astype(BF16)
-            for n in range(2):
-                k = block_at(2 * j + n)
+            for n in range(group):
+                k = block_at(group * j + n)
                 value = both[n * rows:(n + 1) * rows]
                 delta = (k - z + NZ) % NZ
                 way = delta // 5
@@ -364,6 +359,8 @@
                     def _():
                         for copy in part_copies(m, k, way, far):
                             copy.start()
+
+        sq_stage(m)
 
     def hid_sends(m):
         block = hid_all.at[z, part(m)]
@@ -372,13 +369,13 @@
             sign = 1 - 2 * way
             out.append(
                 rdma(
-                    block, relay.at[way, part(m)], az_s.at[m * 4 + 2 + way],
+                    block, relay.at[way, part(m)], az_s,
                     rel_r.at[m * 2 + way], helper(2 * sign),
                 )
             )
             out.append(
                 rdma(
-                    block, block, az_s.at[m * 4 + way], az_r.at[m * 8 + way * 4],
+                    block, block, az_s, az_r.at[m * 8 + way * 4],
                     {"z": (z + sign + NZ) % NZ},
                 )
             )
@@ -387,13 +384,8 @@
     def hid_stage(m):
         rows = SIZES[m]
 
-        @pl.loop(1, NT)
-        def _(i):
-            k = block_at(i)
-            arrived(sq_in.at[m, k], sq_r.at[m * NT + k])
-
-        for slot in range(4):
-            arrived(part_in.at[slot, part(m)], rz_r.at[m * 4 + slot])
+        arrived(sq_in.at[m, pl.ds(0, NZ - 1)], sq_r.at[m])
+        arrived(part_in.at[:, part(m)], rz_r.at[m])
         total = part_own[span_of(m)].astype(F32)
         for slot in range(4):
             total = total + part_in[slot, span_of(m)].astype(F32)
@@ -408,7 +400,7 @@
     def y_copy(m, k):
         return rdma(
             y_out.at[k, part(m)], y_in.at[t, part(m)],
-            rt_s.at[m * NT + k], rt_r.at[m * NT + t], to_tensor((k + z) % NT),
+            rt_s, rt_r.at[m], to_tensor((k + z) % NT),
         )
 
     def down_stage(m):
@@ -450,13 +442,13 @@
                     y_copy(m, k).start()
 
     def core_send(m):
-        return rdma(x_next.at[part(m)], x_all.at[own, part(m)], core_s.at[m], xin_r.at[m], core)
+        return rdma(x_next.at[part(m)], x_all.at[own, part(m)], core_s, xin_r.at[m], core)
 
     def state_send(m):
-        return rdma(x_next.at[part(m)], state_ref.at[0, part(m)], out_s.at[m], out_r.at[m], back)
+        return rdma(x_next.at[part(m)], state_ref.at[0, part(m)], out_s, out_r, back)
 
     def state_here(m):
-        return pltpu.make_async_copy(x_next.at[part(m)], state_ref.at[0, part(m)], out_r.at[m])
+        return pltpu.make_async_copy(x_next.at[part(m)], state_ref.at[0, part(m)], out_r)
 
     def store_state(m):
         @pl.when(moves)
@@ -468,10 +460,7 @@
             state_here(m).start()
 
     def next_stage(m, first_section):
-        @pl.loop(1, NT)
-        def _(i):
-            k = tensor_at(i)
-            arrived(y_in.at[k, part(m)], rt_r.at[m * NT + k])
+        arrived(y_in.at[pl.ds(0, NT - 1), part(m)], rt_r.at[m])
 
         total = x_all[own, span_of(m)].astype(F32)
         for k in range(NT):
@@ -586,66 +575,45 @@
         grad_store.start()
 
     with jax.named_scope("drain"):
+        def left(ref, sem):
+            rdma(ref, ref, sem, gain_r, core).wait_send()
+
         @pl.when(section == 0)
         def _():
-            for m in range(PARTS):
-                core_send(m).wait_send()
+            left(x_next, core_s)
 
         @pl.when(moves & (section == 0))
         def _():
-            for m in range(PARTS):
-                tok_send(m).wait_send()
+            left(x_next, xin_s)
 
         @pl.when(shares_cot)
         def _():
             cot_send.wait_send()
-            for i in range(1, NY + 1):
-                cot_spread(i).wait_send()
+            left(c_all.at[pl.ds(0, NY)], cg_s)
+            left(sq_out, sqh_s)
 
         @pl.when(beside != z)
         def _():
-            for i in range(1, NY):
-                cot_pass(i).wait_send()
+            left(c_all.at[pl.ds(0, NY - 1)], cp_s)
 
         @pl.when(moves)
         def _():
             gain_send.wait_send()
-            for m in range(PARTS):
-                state_send(m).wait_send()
+            left(x_next, out_s)
 
         up_send.wait_send()
         down_send.wait_send()
         grad_send.wait_send()
-
-        @pl.loop(1, NT)
-        def _(i):
-            for m in range(PARTS):
-                spread(m, i).wait_send()
-                sq_spread(m, i).wait_send()
-                y_copy(m, block_at(i)).wait_send()
-
-        @pl.when(shares_cot)
-        def _():
-            for m in range(PARTS):
-                sq_copy(m).wait_send()
-
-        for m in range(PARTS):
-            for way in range(2):
-                for dist in range(1, 4):
-                    k = (z + dist * (1 - 2 * way) + NZ) % NZ
-                    for copy in part_copies(m, k, way, dist):
-                        copy.wait_send()
-                sum_send(m, way).wait_send()
-                for copy in relay_sends(m, way):
-                    copy.wait_send()
-            for copy in part_copies(m, (z + 4) % NZ, 0, 4):
-                copy.wait_send()
-            for copy in hid_sends(m):
-                copy.wait_send()
+        left(x_all.at[pl.ds(0, NT - 1)], ag_s)
+        left(sq_in.at[:, pl.ds(0, NT - 1)], sq_s)
+        left(y_out.at[pl.ds(0, NT - 1)], rt_s)
+        left(part_out.at[pl.ds(0, NZ - 1)], rz_s)
+        left(sum_out, sum_s)
+        left(hid_all.at[pl.ds(0, 4)], az_s)
+        left(hid_all.at[pl.ds(0, 5)], rel_s)
 
     with jax.named_scope("waitstate"):
-        for m in range(PARTS):
-            arrived(state_ref.at[0, part(m)], out_r.at[m])
+        arrived(state_ref.at[0], out_r)
         grad_store.wait()
 
 
@@ -691,11 +659,10 @@
             pltpu.VMEM((hidden, half), BF16),
             pltpu.VMEM((hidden, half), BF16),
         ]
-        + [one] * 14
-        + [dma((8,))] * 2
-        + [dma((PARTS,))] * 7
-        + [dma((8 * PARTS,))] * 6
-        + [dma((n * PARTS,)) for n in (8, 4, 6, 2, 4, 8, 2, 6)]
+        + [one] * 16
+        + [dma((NT,))]
+        + [one] * 12
+        + [dma((n * PARTS,)) for n in (1, 1, 8, 1, 1, 1, 2, 8, 2)]
         + [pltpu.SemaphoreType.REGULAR],
         compiler_params=pltpu.CompilerParams(
             collective_id=0, has_side_effects=True, vmem_limit_bytes=60 * 1024 * 1024

time: 102 us -> 99.2 us (0.973); the launches traced: 100 us -> 98.7 us
  Pallas kernels: 96.5 us -> 94.8 us
    pallas_call x1, Pallas kernels: 96.5 us -> 94.8 us  [body(): pl.pallas_call(run, out_shape=(jax.ShapeDtypeStruct((1, rows, feats), BF1...]
where the time goes in v6:
time: 99.2 us; the launch traced here: 98.7 us
  Pallas kernels  94.8 us (96%)
  local copies, waits for them, and re-layouts  3.29 us (3%)
    pallas_call x1, Pallas kernels, body(): pl.pallas_call(run, out_shape=(jax.ShapeDtypeStruct((1, rows, feats), BF1...  94.8 us
    unnamed x2, local copies, waits for them, and re-layouts  3.29 us

profile of v6, /device:TPU:1, one launch (start us, length us, event | category | flops | bytes accessed | tf_op | source)
XLA Modules:
  0.0 98.7 jit_solution(2817087310994161871)
XLA Ops:
  0.6 94.8 %shard_map.68 = (bf16[1,128,512]{2,1,0:T(8,128)(2,1)}, bf16[1,640,256]{2,1,0:T(8,128)(2,1)}) custom-call(bf16[128,512]{1,0:T(8,128)(2,1)} %refs_0_.1, bf16[1,512]{1,0:T(2,128)(2,1)} %refs_1_.1, bf16[1,256,640]{2,1,0:T(8,128)(2,1)} %refs_2_.1, bf16[1,640,256]{2,1,0:T(8,128)(2,1)} %refs_3_.1, bf16[1,128,4096]{2,1,0:T(8,128)(2,1)} %refs_4_.1), custom_call_target="tpu_custom_call" | custom-call | tf_op jit(solution)/shard_map/pallas_call | solution.py:631
  95.4 1.6 %copy.9 = bf16[1,128,512]{2,1,0:T(8,128)(2,1)} copy(bf16[1,128,512]{2,1,0:T(8,128)(2,1)} %get-tuple-element.4) | data formatting | bytes 262144
  97.0 1.7 %copy.10 = bf16[1,640,256]{2,1,0:T(8,128)(2,1)} copy(bf16[1,640,256]{2,1,0:T(8,128)(2,1)} %get-tuple-element.5) | data formatting | bytes 655360

commit v7 on v6

--- a/solution.py
+++ b/solution.py
@@ -27,18 +27,18 @@
         up1 = 50 + 3 * gap * m
         if section == 0:
             todo += [(up0, "up", m), (up0 + 10, "hid", m), (down0, "down", m)]
-            todo += [(down0 + 6.1, "next", m), (up1 + 4, "sum", m), (up1 + 11.5, "pass", m)]
+            todo += [(down0 + 6.1, "next", m), (up1 + 4, "sum", m), (up1 + 13.1, "pass", m)]
         else:
             todo += [(up0 + 4, "sum", m), (pass0, "pass", m), (up1 - 6.1, "take", m)]
-            todo += [(up1, "up", m), (up1 + 8.5, "hid", m), (up1 + 15.5, "down", m)]
-            todo += [(up1 + 19.5, "next", m)]
+            todo += [(up1, "up", m), (up1 + 9.2, "hid", m), (up1 + 18.3, "down", m)]
+            todo += [(up1 + 23, "next", m)]
     last = 50 + 3 * gap * (PARTS - 1)
     if section == 0:
-        todo += [(18.1, "down_copy", 0), (18.2, "cot_spread", 0), (31, "cot_pass", 0)]
-        todo += [(last + 1, "state", 0), (53.9, "grad", 0)]
+        todo += [(18.1, "down_copy", 0), (25.8, "cot_spread", 0), (37.9, "cot_pass", 0)]
+        todo += [(last + 11, "state", 0), (60.5, "grad", 0)]
     else:
         todo += [(25, "cot_spread", 0), (30.7, "up_copy", 0), (30.8, "cot_pass", 0)]
-        todo += [(last + 0.1, "down_copy", 0), (last + 16, "grad", 0)]
+        todo += [(last + 0.1, "down_copy", 0), (last + 19, "grad", 0)]
     return [(name, m) for _, name, m in sorted(todo)]
 
 
@@ -230,16 +230,16 @@
     def relay_sends(m, way):
         sign = 1 - 2 * way
         block = (z - 2 * sign + NZ) % NZ
-        first = m * 8 + way * 4
+        first = m * 4 - way
         full = relay.at[way, part(m)]
         whole = hid_all.at[block, part(m)]
         return (
             rdma(
                 relay.at[way, side(m, way)], hid_all.at[block, side(m, way)],
-                rel_s, az_r.at[first + 3], helper(2 * sign),
+                rel_s, az_r.at[m * 4 + 3], helper(2 * sign),
             ),
-            rdma(full, whole, rel_s, az_r.at[first + 2], helper(sign)),
-            rdma(full, whole, rel_s, az_r.at[first + 1], core),
+            rdma(full, whole, rel_s, az_r.at[first + 3], helper(sign)),
+            rdma(full, whole, rel_s, az_r.at[first + 2], core),
         )
 
     def pass_stage(m):
@@ -251,7 +251,7 @@
     def spread(m, i):
         return rdma(
             x_all.at[own, part(m)], x_all.at[own, part(m)],
-            ag_s, ag_r.at[m * NT + own], to_tensor(tensor_at(i)),
+            ag_s, ag_r.at[own if m == 0 else NT + 2 * (m - 1) + i // NY], to_tensor(tensor_at(i)),
         )
 
     def sq_copy(m):
@@ -327,13 +327,22 @@
         @pl.loop(0, NT // group)
         def _(j):
             scaled = []
+            if m > 0:
+                @pl.when(j == 0)
+                def _():
+                    arrived(x_all.at[pl.ds(0, NY - 1), part(m)], ag_r.at[NT + 2 * (m - 1)])
+
+                @pl.when(j == 1)
+                def _():
+                    arrived(x_all.at[pl.ds(0, NY), part(m)], ag_r.at[NT + 2 * (m - 1) + 1])
+
             for n in range(group):
                 i = group * j + n
                 k = block_at(i)
-
-                @pl.when(i > 0)
-                def _():
-                    arrived(x_all.at[k, part(m)], ag_r.at[m * NT + k])
+                if m == 0:
+                    @pl.when(i > 0)
+                    def _():
+                        arrived(x_all.at[k, part(m)], ag_r.at[k])
 
                 scaled.append((x_all[k, span_of(m)].astype(F32) * gain_f).astype(BF16))
             both = jnp.dot(
@@ -375,7 +384,7 @@
             )
             out.append(
                 rdma(
-                    block, block, az_s, az_r.at[m * 8 + way * 4],
+                    block, block, az_s, az_r.at[m * 4 + 1 - way],
                     {"z": (z + sign + NZ) % NZ},
                 )
             )
@@ -408,21 +417,15 @@
 
         @pl.loop(0, NZ // 2)
         def _(j):
-            hid = []
-            for i in (2 * j, 2 * j + 1):
-                k = z_at(i)
-
-                @pl.when((i > 0) & (i < NZ - 1))
-                def _():
-                    slot = m * 8 + (i % 2) * 4 + (i + 1) // 2 - 1
-                    arrived(hid_all.at[k, part(m)], az_r.at[slot])
-
-                @pl.when(i == NZ - 1)
-                def _():
-                    for way in range(2):
-                        arrived(hid_all.at[k, side(m, way)], az_r.at[m * 8 + way * 4 + 3])
-
-                hid.append(hid_all[k, span_of(m)])
+            @pl.when(j == 0)
+            def _():
+                arrived(hid_all.at[0, part(m)], az_r.at[m * 4])
+
+            @pl.when(j > 0)
+            def _():
+                arrived(hid_all.at[pl.ds(0, 2), part(m)], az_r.at[m * 4 + j])
+
+            hid = [hid_all[z_at(2 * j + n), span_of(m)] for n in range(2)]
             hid = jnp.concatenate(hid, axis=0)
             y_lo = jnp.dot(hid, down_pair[0], preferred_element_type=F32).astype(BF16)
             y_hi = jnp.dot(hid, down_pair[1], preferred_element_type=F32).astype(BF16)
@@ -662,7 +665,7 @@
         + [one] * 16
         + [dma((NT,))]
         + [one] * 12
-        + [dma((n * PARTS,)) for n in (1, 1, 8, 1, 1, 1, 2, 8, 2)]
+        + [dma((n * PARTS,)) for n in (1, 1, 4, 1, 1, 1, 2, 4, 2)]
         + [pltpu.SemaphoreType.REGULAR],
         compiler_params=pltpu.CompilerParams(
             collective_id=0, has_side_effects=True, vmem_limit_bytes=60 * 1024 * 1024

time: 99.2 us -> 96.5 us (0.973); the launches traced: 98.7 us -> 94.8 us
  Pallas kernels: 94.8 us -> 90.9 us
    pallas_call x1, Pallas kernels: 94.8 us -> 90.9 us  [body(): pl.pallas_call(run, out_shape=(jax.ShapeDtypeStruct((1, rows, feats), BF1...]
where the time goes in v7:
time: 96.5 us; the launch traced here: 94.8 us
  Pallas kernels  90.9 us (94%)
  local copies, waits for them, and re-layouts  3.29 us (3%)
    pallas_call x1, Pallas kernels, body(): pl.pallas_call(run, out_shape=(jax.ShapeDtypeStruct((1, rows, feats), BF1...  90.9 us
    unnamed x2, local copies, waits for them, and re-layouts  3.29 us

profile of v7, /device:TPU:1, one launch (start us, length us, event | category | flops | bytes accessed | tf_op | source)
XLA Modules:
  0.0 94.8 jit_solution(4140684194805943829)
XLA Ops:
  0.6 90.9 %shard_map.68 = (bf16[1,128,512]{2,1,0:T(8,128)(2,1)}, bf16[1,640,256]{2,1,0:T(8,128)(2,1)}) custom-call(bf16[128,512]{1,0:T(8,128)(2,1)} %refs_0_.1, bf16[1,512]{1,0:T(2,128)(2,1)} %refs_1_.1, bf16[1,256,640]{2,1,0:T(8,128)(2,1)} %refs_2_.1, bf16[1,640,256]{2,1,0:T(8,128)(2,1)} %refs_3_.1, bf16[1,128,4096]{2,1,0:T(8,128)(2,1)} %refs_4_.1), custom_call_target="tpu_custom_call" | custom-call | tf_op jit(solution)/shard_map/pallas_call | solution.py:634
  91.5 1.6 %copy.9 = bf16[1,128,512]{2,1,0:T(8,128)(2,1)} copy(bf16[1,128,512]{2,1,0:T(8,128)(2,1)} %get-tuple-element.4) | data formatting | bytes 262144
  93.1 1.7 %copy.10 = bf16[1,640,256]{2,1,0:T(8,128)(2,1)} copy(bf16[1,640,256]{2,1,0:T(8,128)(2,1)} %get-tuple-element.5) | data formatting | bytes 655360

commit v8 on v7

--- a/solution.py
+++ b/solution.py
@@ -34,8 +34,8 @@
             todo += [(up1 + 23, "next", m)]
     last = 50 + 3 * gap * (PARTS - 1)
     if section == 0:
-        todo += [(18.1, "down_copy", 0), (25.8, "cot_spread", 0), (37.9, "cot_pass", 0)]
-        todo += [(last + 11, "state", 0), (60.5, "grad", 0)]
+        todo += [(18.1, "down_copy", 0), (25.8, "cot_spread", 0), (33.2, "cot_pass", 0)]
+        todo += [(last + 14, "state", 0), (60.5, "grad", 0)]
     else:
         todo += [(25, "cot_spread", 0), (30.7, "up_copy", 0), (30.8, "cot_pass", 0)]
         todo += [(last + 0.1, "down_copy", 0), (last + 19, "grad", 0)]

time: 96.5 us -> 95.4 us (0.989)
  no operation moved by 1% of the time
where the time goes in v8:
time: 95.4 us; the launch traced here: 94.5 us
  Pallas kernels  90.6 us (95%)
  local copies, waits for them, and re-layouts  3.29 us (3%)
    pallas_call x1, Pallas kernels, body(): pl.pallas_call(run, out_shape=(jax.ShapeDtypeStruct((1, rows, feats), BF1...  90.6 us
    unnamed x2, local copies, waits for them, and re-layouts  3.29 us

profile of v8, /device:TPU:1, one launch (start us, length us, event | category | flops | bytes accessed | tf_op | source)
XLA Modules:
  0.0 94.5 jit_solution(2427412265856120386)
XLA Ops:
  0.6 90.6 %shard_map.68 = (bf16[1,128,512]{2,1,0:T(8,128)(2,1)}, bf16[1,640,256]{2,1,0:T(8,128)(2,1)}) custom-call(bf16[128,512]{1,0:T(8,128)(2,1)} %refs_0_.1, bf16[1,512]{1,0:T(2,128)(2,1)} %refs_1_.1, bf16[1,256,640]{2,1,0:T(8,128)(2,1)} %refs_2_.1, bf16[1,640,256]{2,1,0:T(8,128)(2,1)} %refs_3_.1, bf16[1,128,4096]{2,1,0:T(8,128)(2,1)} %refs_4_.1), custom_call_target="tpu_custom_call" | custom-call | tf_op jit(solution)/shard_map/pallas_call | solution.py:634
  91.3 1.6 %copy.9 = bf16[1,128,512]{2,1,0:T(8,128)(2,1)} copy(bf16[1,128,512]{2,1,0:T(8,128)(2,1)} %get-tuple-element.4) | data formatting | bytes 262144
  92.8 1.7 %copy.10 = bf16[1,640,256]{2,1,0:T(8,128)(2,1)} copy(bf16[1,640,256]{2,1,0:T(8,128)(2,1)} %get-tuple-element.5) | data formatting | bytes 655360

commit v9 on v8

--- a/solution.py
+++ b/solution.py
@@ -35,7 +35,7 @@
     last = 50 + 3 * gap * (PARTS - 1)
     if section == 0:
         todo += [(18.1, "down_copy", 0), (25.8, "cot_spread", 0), (33.2, "cot_pass", 0)]
-        todo += [(last + 14, "state", 0), (60.5, "grad", 0)]
+        todo += [(last + 14, "state", 0), (63.05, "grad", 0)]
     else:
         todo += [(25, "cot_spread", 0), (30.7, "up_copy", 0), (30.8, "cot_pass", 0)]
         todo += [(last + 0.1, "down_copy", 0), (last + 19, "grad", 0)]

time: 95.4 us -> 96 us (level)
  no operation moved by 1% of the time
where the time goes in v9:
time: 96 us; the launch traced here: 94.7 us
  Pallas kernels  90.8 us (95%)
  local copies, waits for them, and re-layouts  3.29 us (3%)
    pallas_call x1, Pallas kernels, body(): pl.pallas_call(run, out_shape=(jax.ShapeDtypeStruct((1, rows, feats), BF1...  90.8 us
    unnamed x2, local copies, waits for them, and re-layouts  3.29 us

profile of v9, /device:TPU:1, one launch (start us, length us, event | category | flops | bytes accessed | tf_op | source)
XLA Modules:
  0.0 94.7 jit_solution(13763514342402587825)
XLA Ops:
  0.6 90.8 %shard_map.68 = (bf16[1,128,512]{2,1,0:T(8,128)(2,1)}, bf16[1,640,256]{2,1,0:T(8,128)(2,1)}) custom-call(bf16[128,512]{1,0:T(8,128)(2,1)} %refs_0_.1, bf16[1,512]{1,0:T(2,128)(2,1)} %refs_1_.1, bf16[1,256,640]{2,1,0:T(8,128)(2,1)} %refs_2_.1, bf16[1,640,256]{2,1,0:T(8,128)(2,1)} %refs_3_.1, bf16[1,128,4096]{2,1,0:T(8,128)(2,1)} %refs_4_.1), custom_call_target="tpu_custom_call" | custom-call | tf_op jit(solution)/shard_map/pallas_call | solution.py:634
  91.4 1.6 %copy.9 = bf16[1,128,512]{2,1,0:T(8,128)(2,1)} copy(bf16[1,128,512]{2,1,0:T(8,128)(2,1)} %get-tuple-element.4) | data formatting | bytes 262144
  93.0 1.7 %copy.10 = bf16[1,640,256]{2,1,0:T(8,128)(2,1)} copy(bf16[1,640,256]{2,1,0:T(8,128)(2,1)} %get-tuple-element.5) | data formatting | bytes 655360
